TPU v7x, 256 devices: a whole 4x4x8 slice. The times are simulated.
256 devices in a mesh: gx: 32 (over y, z), gy: 8 (over x, core).
Axes of the slice: x: 4, y: 4, z: 8, core: 2. Of those that a mesh axis runs over, the one named last changes fastest.
Arguments:
- modes: float32 [16, 3, 128, 64, 128], P(None, None, 'gx', 'gy'), may hold values from -0.03 to 0.03
- region: int32 [128, 64, 128], P('gx', 'gy'), may hold values from 0 to 15
- stiffness: float32 [16], replicated, may hold values from 0.1 to 10
- coarse_group: int32 [32, 8], replicated, may hold values from 0 to 3
Outputs:
- coarse: float32 [32, 64, 192], P('gx', 'gy')
All inputs are finite; a program needn't handle non-finite values.
Results may differ from a plain program's by a relative error of at most 0.0003.
Values sent between devices are 32-bit elements; how exact they have to be, the bound alone decides.
No kernel may reach another device: no remote copies, remote signals or barrier semaphores. Data moves between devices by JAX's collectives and lax.ppermute only.
A program may use at most 128 MiB of HBM per device.

v0:
```python
import jax
import jax.numpy as jnp
from jax import lax
from jax.sharding import PartitionSpec as P

GROUPS = 4


beta_shear = 0.5
mass_share = 0.1


def extended(cells, sides, width):
    for axis, dim in sides:
        count = lax.axis_size(axis)
        ends = count - 1
        head = lax.slice_in_dim(cells, 0, width, axis=dim)
        tail = lax.slice_in_dim(cells, cells.shape[dim] - width, cells.shape[dim], axis=dim)
        cells = jnp.concatenate(
            [
                lax.ppermute(tail, axis, [(i, (i + 1) % count) for i in range(ends)]),
                cells,
                lax.ppermute(head, axis, [((i + 1) % count, i) for i in range(ends)]),
            ],
            axis=dim,
        )
    return cells


def in_blocks(array, dim, peers):
    before, after = (array.shape[:dim], array.shape[dim + 1 :])
    return jnp.moveaxis(array.reshape(*before, peers, -1, *after), dim, 0)


def sum_at_owner(array, axis, dim):
    peers = lax.axis_size(axis)
    blocks = lax.all_to_all(in_blocks(array, dim, peers), axis, 0, 0, tiled=True)
    return jnp.sum(blocks, axis=0)


def all_offsets():
    return [
        (shift_x, shift_y, shift_z)
        for shift_x in (-1, 0, 1)
        for shift_y in (-1, 0, 1)
        for shift_z in (-1, 0, 1)
        if (shift_x, shift_y, shift_z) != (0, 0, 0)
    ]


def apply_operator(padded, stiff_pad):
    span_x = padded.shape[2] - 2
    span_y = padded.shape[3] - 2
    span_z = padded.shape[4] - 2
    centre = padded[:, :, 1 : span_x + 1, 1 : span_y + 1, 1 : span_z + 1]
    stiff_here = stiff_pad[1 : span_x + 1, 1 : span_y + 1, 1 : span_z + 1]
    result = mass_share * stiff_here * centre
    for step_x, step_y, step_z in all_offsets():
        reach_len = abs(step_x) + abs(step_y) + abs(step_z)
        weight = 0.5 ** (reach_len - 1)
        nearby = padded[
            :,
            :,
            1 + step_x : 1 + step_x + span_x,
            1 + step_y : 1 + step_y + span_y,
            1 + step_z : 1 + step_z + span_z,
        ]
        stiff_there = stiff_pad[
            1 + step_x : 1 + step_x + span_x,
            1 + step_y : 1 + step_y + span_y,
            1 + step_z : 1 + step_z + span_z,
        ]
        coupling = 0.5 * weight * (stiff_here + stiff_there)
        differ = centre - nearby
        along_dir = (
            beta_shear
            / reach_len
            * (step_x * differ[:, 0] + step_y * differ[:, 1] + step_z * differ[:, 2])
        )
        pushed = differ + jnp.stack(
            [step_x * along_dir, step_y * along_dir, step_z * along_dir], axis=1
        )
        result = result + coupling * pushed
    return result


def contract(left_side, right_side):
    return jnp.einsum("kaxyz,jaxyz->kj", left_side, right_side, precision=lax.Precision.HIGHEST)


def pair_blocks(applied, mode_cycle):
    span_x = mode_cycle.shape[2] - 2
    span_y = mode_cycle.shape[3] - 2
    bounds_x = [(0, 1), (1, span_x + 1), (span_x + 1, span_x + 2)]
    bounds_y = [(0, 1), (1, span_y + 1), (span_y + 1, span_y + 2)]
    rows_out = []
    for low_x, high_x in bounds_x:
        cols_out = []
        for low_y, high_y in bounds_y:
            cols_out.append(
                contract(
                    applied[:, :, low_x:high_x, low_y:high_y],
                    mode_cycle[:, :, low_x:high_x, low_y:high_y],
                )
            )
        rows_out.append(jnp.stack(cols_out))
    return jnp.stack(rows_out)


def shards(modes, region, stiffness, coarse_group):
    width = modes.shape[0]
    levels = jnp.arange(stiffness.shape[0], dtype=jnp.int32)
    stiff_cells = jnp.sum(jnp.where(region[..., None] == levels, stiffness, 0.0), axis=-1)
    stiff_cycle = extended(stiff_cells, (("gx", 0), ("gy", 1)), 1)
    stiff_pad = jnp.pad(stiff_cycle, ((1, 1), (1, 1), (1, 1)))
    padded = jnp.pad(modes, ((0, 0), (0, 0), (2, 2), (2, 2), (1, 1)))
    applied = apply_operator(padded, stiff_pad)
    group_pad = jnp.pad(coarse_group, 1, constant_values=-1)
    neighbours = lax.dynamic_slice(group_pad, (lax.axis_index("gx"), lax.axis_index("gy")), (3, 3))
    labels = jnp.arange(GROUPS, dtype=jnp.int32)
    hot_near = (neighbours[..., None] == labels).astype(jnp.float32)
    hot_self = hot_near[1, 1]
    mode_cycle = extended(modes, (("gx", 2), ("gy", 3)), 1)
    pair_nine = pair_blocks(applied, mode_cycle)
    partial_value = jnp.einsum(
        "g,xykj,xyh->gkxhj", hot_self, pair_nine, hot_near, precision=lax.Precision.HIGHEST
    )
    partial_value = partial_value.reshape(GROUPS * width, 3 * GROUPS * width)
    coarse_rows = sum_at_owner(partial_value, "gy", 0)
    return coarse_rows[None]


def solution(mesh):
    in_specs = (P(None, None, "gx", "gy", None), P("gx", "gy", None), P(), P())
    out_specs = P("gx", "gy", None)
    return jax.shard_map(shards, mesh=mesh, in_specs=in_specs, out_specs=out_specs, check_vma=False)
```

profile of v0, /device:TPU:24, one launch (start us, length us, event | category | flops | bytes accessed | tf_op | source)
XLA Modules:
  0.0 115.4 jit_solution(1312930369968259804)
XLA Ops:
  0.0 0.9 select_reduce_fusion
  0.9 3.8 %collective-permute-start = (f32[1,8,128]{2,1,0:T(8,128)S(1)}, f32[1,8,128]{2,1,0:T(8,128)S(1)}, u32[]{:S(2)}, u32[]{:S(2)}) collective-permute-start(f32[1,8,128]{2,1,0:T(8,128)S(1)} %get-tuple-element.129), channel_id=1, source_target_pairs={{0,8},{8,16},{16,24},{24,32},{32,40},{40,48},{48,56},{56,64},{64,7... | collective-permute-start | bytes 12296 | tf_op jit(solution)/shard_map/ppermute | solution.py:21
  4.7 6.0 %collective-permute-start.1 = (f32[1,8,128]{2,1,0:T(8,128)S(1)}, f32[1,8,128]{2,1,0:T(8,128)S(1)}, u32[]{:S(2)}, u32[]{:S(2)}) collective-permute-start(f32[1,8,128]{2,1,0:T(8,128)S(1)} %get-tuple-element.130), channel_id=1, source_target_pairs={{8,0},{16,8},{24,16},{32,24},{40,32},{48,40},{56,48},{64,56},{72,6... | collective-permute-start | bytes 12296 | tf_op jit(solution)/shard_map/ppermute | solution.py:23
  10.8 1.6 %copy.42 = f32[16,3,4,8,128]{4,0,1,3,2:T(8,128)S(1)} copy(f32[16,3,4,8,128]{4,3,2,1,0:T(8,128)} %param.4) | data formatting | bytes 1572864 | tf_op args[0]
  12.4 0.8 fusion.182
  13.1 1.9 %collective-permute-start.4 = (f32[16,3,1,8,128]{4,0,1,3,2:T(8,128)}, f32[16,3,1,8,128]{4,0,1,3,2:T(8,128)S(1)}, u32[]{:S(2)}, u32[]{:S(2)}) collective-permute-start(f32[16,3,1,8,128]{4,0,1,3,2:T(8,128)} %get-tuple-element.86), channel_id=1, source_target_pairs={{0,8},{8,16},{16,24},{24,32},{32,40},{40,48},{48,56},{56,64},{64,7... | collective-permute-start | bytes 589832 | tf_op jit(solution)/shard_map/ppermute | solution.py:21
  15.1 6.0 %collective-permute-start.5 = (f32[16,3,1,8,128]{4,0,1,3,2:T(8,128)}, f32[16,3,1,8,128]{4,0,1,3,2:T(8,128)}, u32[]{:S(2)}, u32[]{:S(2)}) collective-permute-start(f32[16,3,1,8,128]{4,0,1,3,2:T(8,128)} %get-tuple-element.85), channel_id=1, source_target_pairs={{8,0},{16,8},{24,16},{32,24},{40,32},{48,40},{56,48},{64,56},{72,6... | collective-permute-start | bytes 589832 | tf_op jit(solution)/shard_map/ppermute | solution.py:23
  21.1 9.9 %fusion = (f32[16,3,6,10,128]{4,0,1,3,2:T(8,128)}, f32[16,3,6,10,128]{4,0,1,3,2:T(8,128)}, f32[16,3,6,10,128]{4,0,1,3,2:T(8,128)}, f32[16,3,6,10,128]{4,0,1,3,2:...) fusion(f32[16,3,4,8,128]{4,0,1,3,2:T(8,128)S(1)} %copy.42), kind=kLoop, calls=%fused_computation.27 | loop fusion | flops 7004160 | bytes 28803072 | tf_op jit(solution)/shard_map/sub | solution.py:74
  31.1 3.3 %fusion.25 = (f32[16,3,6,10,128]{4,0,1,3,2:T(8,128)}, f32[16,3,6,10,128]{4,0,1,3,2:T(8,128)S(1)}, f32[16,3,6,10,128]{4,0,1,3,2:T(8,128)S(1)}, f32[16,3,6,10,128]...) fusion(f32[16,3,4,8,128]{4,0,1,3,2:T(8,128)S(1)} %copy.42), kind=kLoop, calls=%fused_computation.52 | loop fusion | flops 2580480 | bytes 11108352 | tf_op jit(solution)/shard_map/sub | solution.py:74
  34.6 1.1 broadcast_multiply_fusion.44
  35.7 1.0 broadcast_multiply_fusion.10
  36.8 1.2 %broadcast_multiply_fusion.37 = (f32[16,1,6,10,128]{4,0,1,3,2:T(8,128)}, f32[16,1,6,10,128]{4,0,1,3,2:T(8,128)}, f32[16,1,6,10,128]{4,0,1,3,2:T(8,128)}, f32[16,1,6,10,128]{4,0,1,3,2:T(8,128)S(1)}) fusion(f32[16,3,6,10,128]{4,0,1,3,2:T(8,128)S(1)} %copy-done.15, f32[16,3,6,10,128]{4,0,1,3,2:T(8,128)S(1)} %copy-done.14), kind=kLoop, calls=%fused_computation.303 | loop fusion | flops 1351680 | bytes 4915200 | tf_op jit(solution)/shard_map/mul | solution.py:81
  38.0 1.0 broadcast_multiply_fusion.24
  39.0 0.8 copy-done.12
  39.8 1.2 %broadcast_multiply_fusion.35 = (f32[16,1,6,10,128]{4,0,1,3,2:T(8,128)}, f32[16,1,6,10,128]{4,0,1,3,2:T(8,128)S(1)}, f32[16,1,6,10,128]{4,0,1,3,2:T(8,128)}, f32[16,1,6,10,128]{4,0,1,3,2:T(8,128)}) fusion(f32[16,3,6,10,128]{4,0,1,3,2:T(8,128)S(1)} %copy-done.13, f32[16,3,6,10,128]{4,0,1,3,2:T(8,128)S(1)} %copy-done.12), kind=kLoop, calls=%fused_computation.301 | loop fusion | flops 1228800 | bytes 4915200 | tf_op jit(solution)/shard_map/mul | solution.py:81
  41.1 1.1 broadcast_multiply_fusion.8
  42.1 1.2 %broadcast_multiply_fusion.1 = (f32[16,1,6,10,128]{4,0,1,3,2:T(8,128)}, f32[16,1,6,10,128]{4,0,1,3,2:T(8,128)}, f32[16,1,6,10,128]{4,0,1,3,2:T(8,128)}, f32[16,1,6,10,128]{4,0,1,3,2:T(8,128)S(1)}) fusion(f32[16,3,6,10,128]{4,0,1,3,2:T(8,128)S(1)} %get-tuple-element.74, f32[16,3,6,10,128]{4,0,1,3,2:T(8,128)S(1)} %get-tuple-element.77), kind=kLoop, calls=%fused_computation.267 | loop fusion | flops 1351680 | bytes 4915200 | tf_op jit(solution)/shard_map/mul | solution.py:76
  43.3 1.0 broadcast_multiply_fusion.22
  44.4 1.3 %broadcast_multiply_fusion.5 = (f32[16,1,6,10,128]{4,0,1,3,2:T(8,128)}, f32[16,1,6,10,128]{4,0,1,3,2:T(8,128)S(1)}, f32[16,1,6,10,128]{4,0,1,3,2:T(8,128)}, f32[16,1,6,10,128]{4,0,1,3,2:T(8,128)}) fusion(f32[16,3,6,10,128]{4,0,1,3,2:T(8,128)S(1)} %get-tuple-element.80, f32[16,3,6,10,128]{4,0,1,3,2:T(8,128)S(1)} %get-tuple-element.79), kind=kLoop, calls=%fused_computation.271 | loop fusion | flops 1228800 | bytes 4915200 | tf_op jit(solution)/shard_map/mul | solution.py:76
  45.7 1.0 broadcast_multiply_fusion.31
  46.9 3.4 %broadcast_multiply_fusion.13 = (f32[16,1,6,10,128]{4,0,1,3,2:T(8,128)}, f32[16,1,6,10,128]{4,0,1,3,2:T(8,128)}, f32[16,1,6,10,128]{4,0,1,3,2:T(8,128)}, f32[16,1,6,10,128]{4,0,1,3,2:T(8,128)}) fusion(f32[16,3,6,10,128]{4,0,1,3,2:T(8,128)} %get-tuple-element.69, f32[16,3,6,10,128]{4,0,1,3,2:T(8,128)} %get-tuple-element.63), kind=kLoop, calls=%fused_computation.279 | loop fusion | flops 1720320 | bytes 4915200 | tf_op jit(solution)/shard_map/mul | solution.py:81
  50.3 1.4 %broadcast_multiply_fusion.18 = (f32[16,1,6,10,128]{4,0,1,3,2:T(8,128)}, f32[16,1,6,10,128]{4,0,1,3,2:T(8,128)}, f32[16,1,6,10,128]{4,0,1,3,2:T(8,128)}, f32[16,1,6,10,128]{4,0,1,3,2:T(8,128)}) fusion(f32[16,3,6,10,128]{4,0,1,3,2:T(8,128)S(1)} %copy-done.11, f32[16,3,6,10,128]{4,0,1,3,2:T(8,128)S(1)} %copy-done.10), kind=kLoop, calls=%fused_computation.284 | loop fusion | flops 1228800 | bytes 4915200 | tf_op jit(solution)/shard_map/mul | solution.py:81
  51.7 0.7 copy-done.8
  52.3 0.4 copy-done.9
  52.8 1.4 %broadcast_multiply_fusion.42 = (f32[16,1,6,10,128]{4,0,1,3,2:T(8,128)}, f32[16,1,6,10,128]{4,0,1,3,2:T(8,128)}, f32[16,1,6,10,128]{4,0,1,3,2:T(8,128)}, f32[16,1,6,10,128]{4,0,1,3,2:T(8,128)}) fusion(f32[16,3,6,10,128]{4,0,1,3,2:T(8,128)S(1)} %copy-done.9, f32[16,3,6,10,128]{4,0,1,3,2:T(8,128)S(1)} %copy-done.8), kind=kLoop, calls=%fused_computation.308 | loop fusion | flops 1720320 | bytes 4915200 | tf_op jit(solution)/shard_map/mul | solution.py:81
  54.2 0.7 copy-done.6
  55.3 1.4 %broadcast_multiply_fusion.29 = (f32[16,1,6,10,128]{4,0,1,3,2:T(8,128)}, f32[16,1,6,10,128]{4,0,1,3,2:T(8,128)}, f32[16,1,6,10,128]{4,0,1,3,2:T(8,128)}, f32[16,1,6,10,128]{4,0,1,3,2:T(8,128)}) fusion(f32[16,3,6,10,128]{4,0,1,3,2:T(8,128)S(1)} %copy-done.6, f32[16,3,6,10,128]{4,0,1,3,2:T(8,128)S(1)} %copy-done.7), kind=kLoop, calls=%fused_computation.295 | loop fusion | flops 1351680 | bytes 4915200 | tf_op jit(solution)/shard_map/mul | solution.py:81
  56.7 0.7 copy-done.4
  57.8 1.5 %broadcast_multiply_fusion.50 = (f32[16,1,6,10,128]{4,0,1,3,2:T(8,128)}, f32[16,1,6,10,128]{4,0,1,3,2:T(8,128)}, f32[16,1,6,10,128]{4,0,1,3,2:T(8,128)}, f32[16,1,6,10,128]{4,0,1,3,2:T(8,128)}) fusion(f32[16,3,6,10,128]{4,0,1,3,2:T(8,128)S(1)} %copy-done.5, f32[16,3,6,10,128]{4,0,1,3,2:T(8,128)S(1)} %copy-done.4), kind=kLoop, calls=%fused_computation.316 | loop fusion | flops 1474560 | bytes 4915200 | tf_op jit(solution)/shard_map/mul | solution.py:76
  59.3 0.6 copy-done.18
  60.4 1.2 %fusion.78 = (f32[16,6,10,128]{3,0,2,1:T(8,128)}, f32[16,6,10,128]{3,0,2,1:T(8,128)}) fusion(f32[16,3,6,10,128]{4,0,1,3,2:T(8,128)S(1)} %copy-done.19, f32[16,3,6,10,128]{4,0,1,3,2:T(8,128)S(1)} %copy-done.18), kind=kLoop, calls=%fused_computation.165 | loop fusion | flops 737280 | bytes 3932160 | tf_op jit(solution)/shard_map/stack | solution.py:80
  61.5 0.6 copy-done.2
  62.6 1.4 %broadcast_multiply_fusion.30 = (f32[16,1,6,10,128]{4,0,1,3,2:T(8,128)}, f32[16,1,6,10,128]{4,0,1,3,2:T(8,128)}, f32[16,1,6,10,128]{4,0,1,3,2:T(8,128)}, f32[16,1,6,10,128]{4,0,1,3,2:T(8,128)}) fusion(f32[16,3,6,10,128]{4,0,1,3,2:T(8,128)S(1)} %copy-done.2, f32[16,3,6,10,128]{4,0,1,3,2:T(8,128)S(1)} %copy-done.3), kind=kLoop, calls=%fused_computation.296 | loop fusion | flops 1228800 | bytes 4915200 | tf_op jit(solution)/shard_map/mul | solution.py:81
  64.0 0.6 copy-done.1
  64.7 1.4 %broadcast_multiply_fusion = (f32[16,1,6,10,128]{4,0,1,3,2:T(8,128)}, f32[16,1,6,10,128]{4,0,1,3,2:T(8,128)}, f32[16,1,6,10,128]{4,0,1,3,2:T(8,128)}, f32[16,1,6,10,128]{4,0,1,3,2:T(8,128)}) fusion(f32[16,3,6,10,128]{4,0,1,3,2:T(8,128)S(1)} %get-tuple-element.81, f32[16,3,6,10,128]{4,0,1,3,2:T(8,128)S(1)} %copy-done.1), kind=kLoop, calls=%fused_computation.266 | loop fusion | flops 1351680 | bytes 4915200 | tf_op jit(solution)/shard_map/mul | solution.py:76
  66.2 1.6 %collective-permute-start.2 = (f32[6,1,128]{2,1,0:T(1,128)S(1)}, f32[6,1,128]{2,1,0:T(1,128)S(1)}, u32[]{:S(2)}, u32[]{:S(2)}) collective-permute-start(f32[6,1,128]{2,1,0:T(1,128)S(1)} %get-tuple-element.127), channel_id=1, source_target_pairs={{0,1},{1,2},{2,3},{3,4},{4,5},{5,6},{6,7},{8,9},{9,10},{10,11},{11... | collective-permute-start | bytes 9224 | tf_op jit(solution)/shard_map/ppermute | solution.py:21
  67.8 1.3 %collective-permute-start.3 = (f32[6,1,128]{2,1,0:T(1,128)S(1)}, f32[6,1,128]{2,1,0:T(1,128)S(1)}, u32[]{:S(2)}, u32[]{:S(2)}) collective-permute-start(f32[6,1,128]{2,1,0:T(1,128)S(1)} %get-tuple-element.128), channel_id=1, source_target_pairs={{1,0},{2,1},{3,2},{4,3},{5,4},{6,5},{7,6},{9,8},{10,9},{11,10},{12... | collective-permute-start | bytes 9224 | tf_op jit(solution)/shard_map/ppermute | solution.py:23
  69.1 3.5 %collective-permute-done.3 = f32[6,1,128]{2,1,0:T(1,128)S(1)} collective-permute-done((f32[6,1,128]{2,1,0:T(1,128)S(1)}, f32[6,1,128]{2,1,0:T(1,128)S(1)}, u32[]{:S(2)}, u32[]{:S(2)}) %collective-permute-start.3) | collective-permute-done | bytes 3104 | tf_op jit(solution)/shard_map/ppermute | solution.py:23
  73.1 16.2 %fusion.74 = f32[16,3,6,10,128]{4,0,1,3,2:T(8,128)S(1)} fusion(f32[16,1,6,10,128]{4,0,1,3,2:T(8,128)} %get-tuple-element.131, f32[16,1,6,10,128]{4,0,1,3,2:T(8,128)} %get-tuple-element.132, f32[16,1,6,10,128]{4,0,1,3,2:T(8,128)} %get-tuple-element.135, f32[16,1,6,10,128]{4,0,1,3,2:T(8,128)} %get-tuple-element.136, ...), kind=kLoop, calls=%fused_computation.125 | loop fusion | flops 56401920 | bytes 30615552 | tf_op jit(solution)/shard_map/add | solution.py:83
  89.4 1.1 copy-done
  90.5 1.4 %convolution_bitcast_fusion = f32[1,16,16]{2,1,0:T(8,128)S(1)} fusion(f32[16,3,4,8,128]{4,3,2,1,0:T(8,128)S(1)} %copy-done, f32[16,3,6,10,128]{4,0,1,3,2:T(8,128)S(1)} %fusion.74), kind=kOutput, calls=%fused_computation.126 | convolution fusion | flops 37748736 | bytes 1573888 | tf_op jit(solution)/shard_map/kaxyz,jaxyz->kj/dot_general | solution.py:88
  91.9 0.5 constant_dynamic-update-slice_fusion.1
  92.4 0.9 constant_dynamic-update-slice_fusion
  93.4 4.3 %collective-permute-start.6 = (f32[16,3,6,1,128]{4,0,1,3,2:T(8,128)S(1)}, f32[16,3,6,1,128]{4,0,1,3,2:T(8,128)S(1)}, u32[]{:S(2)}, u32[]{:S(2)}) collective-permute-start(f32[16,3,6,1,128]{4,0,1,3,2:T(8,128)S(1)} %get-tuple-element.57), channel_id=1, source_target_pairs={{0,1},{1,2},{2,3},{3,4},{4,5},{5,6},{6,7},{8,9},{9,10},{10,11},{11... | collective-permute-start | bytes 442376 | tf_op jit(solution)/shard_map/ppermute | solution.py:21
  97.6 1.3 %collective-permute-start.7 = (f32[16,3,6,1,128]{4,0,1,3,2:T(8,128)S(1)}, f32[16,3,6,1,128]{4,0,1,3,2:T(8,128)S(1)}, u32[]{:S(2)}, u32[]{:S(2)}) collective-permute-start(f32[16,3,6,1,128]{4,0,1,3,2:T(8,128)S(1)} %get-tuple-element.58), channel_id=1, source_target_pairs={{1,0},{2,1},{3,2},{4,3},{5,4},{6,5},{7,6},{9,8},{10,9},{11,10},{12... | collective-permute-start | bytes 442376 | tf_op jit(solution)/shard_map/ppermute | solution.py:23
  99.3 1.3 %convolution_bitcast_fusion.7 = f32[1,16,16]{2,1,0:T(8,128)S(1)} fusion(f32[16,3,8,128]{3,0,1,2:T(8,128)S(1)} %get-tuple-element.18, f32[16,3,1,8,128]{4,0,1,3,2:T(8,128)} %collective-permute-done.5), kind=kOutput, calls=%fused_computation.133 | convolution fusion | flops 9437184 | bytes 394240 | tf_op jit(solution)/shard_map/kaxyz,jaxyz->kj/dot_general | solution.py:88
  102.6 12.3 %all_to_all.5 = f32[8,8,192]{2,1,0:T(8,128)S(1)} all-to-all(f32[8,8,192]{2,1,0:T(8,128)S(1)} %reshape_reshape.3), channel_id=1, replica_groups=mesh['gx'=32,'gy'=8] {'gy'}, dimensions={0} | all-to-all | bytes 98304 | tf_op jit(solution)/shard_map/all_to_all | solution.py:37
  114.8 0.6 reduce_sum.19
  (106 shorter events, 5.2 us)
Async XLA Ops:
  0.9 65.3 %collective-permute-start = (f32[1,8,128]{2,1,0:T(8,128)S(1)}, f32[1,8,128]{2,1,0:T(8,128)S(1)}, u32[]{:S(2)}, u32[]{:S(2)}) collective-permute-start(f32[1,8,128]{2,1,0:T(8,128)S(1)} %get-tuple-element.129), channel_id=1, source_target_pairs={{0,8},{8,16},{16,24},{24,32},{32,40},{40,48},{48,56},{56,64},{64,7... | collective-permute-start | bytes 12296 | tf_op jit(solution)/shard_map/ppermute | solution.py:21
  4.7 61.5 %collective-permute-start.1 = (f32[1,8,128]{2,1,0:T(8,128)S(1)}, f32[1,8,128]{2,1,0:T(8,128)S(1)}, u32[]{:S(2)}, u32[]{:S(2)}) collective-permute-start(f32[1,8,128]{2,1,0:T(8,128)S(1)} %get-tuple-element.130), channel_id=1, source_target_pairs={{8,0},{16,8},{24,16},{32,24},{40,32},{48,40},{56,48},{64,56},{72,6... | collective-permute-start | bytes 12296 | tf_op jit(solution)/shard_map/ppermute | solution.py:23
  13.1 78.7 %collective-permute-start.4 = (f32[16,3,1,8,128]{4,0,1,3,2:T(8,128)}, f32[16,3,1,8,128]{4,0,1,3,2:T(8,128)S(1)}, u32[]{:S(2)}, u32[]{:S(2)}) collective-permute-start(f32[16,3,1,8,128]{4,0,1,3,2:T(8,128)} %get-tuple-element.86), channel_id=1, source_target_pairs={{0,8},{8,16},{16,24},{24,32},{32,40},{40,48},{48,56},{56,64},{64,7... | collective-permute-start | bytes 589832 | tf_op jit(solution)/shard_map/ppermute | solution.py:21
  15.1 77.3 %collective-permute-start.5 = (f32[16,3,1,8,128]{4,0,1,3,2:T(8,128)}, f32[16,3,1,8,128]{4,0,1,3,2:T(8,128)}, u32[]{:S(2)}, u32[]{:S(2)}) collective-permute-start(f32[16,3,1,8,128]{4,0,1,3,2:T(8,128)} %get-tuple-element.85), channel_id=1, source_target_pairs={{8,0},{16,8},{24,16},{32,24},{40,32},{48,40},{56,48},{64,56},{72,6... | collective-permute-start | bytes 589832 | tf_op jit(solution)/shard_map/ppermute | solution.py:23
  31.1 3.3 %copy-start.16 = (f32[16,3,6,10,128]{4,0,1,3,2:T(8,128)S(1)}, f32[16,3,6,10,128]{4,0,1,3,2:T(8,128)}, u32[]{:S(2)}) copy-start(f32[16,3,6,10,128]{4,0,1,3,2:T(8,128)} %get-tuple-element.64) | copy-start | bytes 4423684
  31.1 3.3 %copy-start.17 = (f32[16,3,6,10,128]{4,0,1,3,2:T(8,128)S(1)}, f32[16,3,6,10,128]{4,0,1,3,2:T(8,128)}, u32[]{:S(2)}) copy-start(f32[16,3,6,10,128]{4,0,1,3,2:T(8,128)} %get-tuple-element.66) | copy-start | bytes 4423684
  34.6 2.2 %copy-start.14 = (f32[16,3,6,10,128]{4,0,1,3,2:T(8,128)S(1)}, f32[16,3,6,10,128]{4,0,1,3,2:T(8,128)}, u32[]{:S(2)}) copy-start(f32[16,3,6,10,128]{4,0,1,3,2:T(8,128)} %get-tuple-element.70) | copy-start | bytes 4423684
  34.6 2.2 %copy-start.15 = (f32[16,3,6,10,128]{4,0,1,3,2:T(8,128)S(1)}, f32[16,3,6,10,128]{4,0,1,3,2:T(8,128)}, u32[]{:S(2)}) copy-start(f32[16,3,6,10,128]{4,0,1,3,2:T(8,128)} %get-tuple-element.71) | copy-start | bytes 4423684
  36.7 2.3 %copy-start.13 = (f32[16,3,6,10,128]{4,0,1,3,2:T(8,128)S(1)}, f32[16,3,6,10,128]{4,0,1,3,2:T(8,128)}, u32[]{:S(2)}) copy-start(f32[16,3,6,10,128]{4,0,1,3,2:T(8,128)} %get-tuple-element.73) | copy-start | bytes 4423684
  38.0 1.8 %copy-start.12 = (f32[16,3,6,10,128]{4,0,1,3,2:T(8,128)S(1)}, f32[16,3,6,10,128]{4,0,1,3,2:T(8,128)}, u32[]{:S(2)}) copy-start(f32[16,3,6,10,128]{4,0,1,3,2:T(8,128)} %get-tuple-element.72) | copy-start | bytes 4423684
  45.7 1.0 copy-start.39
  46.9 3.4 %copy-start.10 = (f32[16,3,6,10,128]{4,0,1,3,2:T(8,128)S(1)}, f32[16,3,6,10,128]{4,0,1,3,2:T(8,128)}, u32[]{:S(2)}) copy-start(f32[16,3,6,10,128]{4,0,1,3,2:T(8,128)} %get-tuple-element.61) | copy-start | bytes 4423684
  46.9 3.4 %copy-start.11 = (f32[16,3,6,10,128]{4,0,1,3,2:T(8,128)S(1)}, f32[16,3,6,10,128]{4,0,1,3,2:T(8,128)}, u32[]{:S(2)}) copy-start(f32[16,3,6,10,128]{4,0,1,3,2:T(8,128)} %get-tuple-element.67) | copy-start | bytes 4423684
  50.3 2.1 %copy-start.8 = (f32[16,3,6,10,128]{4,0,1,3,2:T(8,128)S(1)}, f32[16,3,6,10,128]{4,0,1,3,2:T(8,128)}, u32[]{:S(2)}) copy-start(f32[16,3,6,10,128]{4,0,1,3,2:T(8,128)} %get-tuple-element.62) | copy-start | bytes 4423684
  50.3 2.5 %copy-start.9 = (f32[16,3,6,10,128]{4,0,1,3,2:T(8,128)S(1)}, f32[16,3,6,10,128]{4,0,1,3,2:T(8,128)}, u32[]{:S(2)}) copy-start(f32[16,3,6,10,128]{4,0,1,3,2:T(8,128)} %get-tuple-element.68) | copy-start | bytes 4423684
  52.8 2.1 %copy-start.6 = (f32[16,3,6,10,128]{4,0,1,3,2:T(8,128)S(1)}, f32[16,3,6,10,128]{4,0,1,3,2:T(8,128)}, u32[]{:S(2)}) copy-start(f32[16,3,6,10,128]{4,0,1,3,2:T(8,128)} %get-tuple-element.60) | copy-start | bytes 4423684
  52.8 2.5 %copy-start.7 = (f32[16,3,6,10,128]{4,0,1,3,2:T(8,128)S(1)}, f32[16,3,6,10,128]{4,0,1,3,2:T(8,128)}, u32[]{:S(2)}) copy-start(f32[16,3,6,10,128]{4,0,1,3,2:T(8,128)} %get-tuple-element.75) | copy-start | bytes 4423684
  55.3 2.1 %copy-start.4 = (f32[16,3,6,10,128]{4,0,1,3,2:T(8,128)S(1)}, f32[16,3,6,10,128]{4,0,1,3,2:T(8,128)}, u32[]{:S(2)}) copy-start(f32[16,3,6,10,128]{4,0,1,3,2:T(8,128)} %get-tuple-element.65) | copy-start | bytes 4423684
  55.3 2.5 %copy-start.5 = (f32[16,3,6,10,128]{4,0,1,3,2:T(8,128)S(1)}, f32[16,3,6,10,128]{4,0,1,3,2:T(8,128)}, u32[]{:S(2)}) copy-start(f32[16,3,6,10,128]{4,0,1,3,2:T(8,128)} %get-tuple-element.76) | copy-start | bytes 4423684
  57.8 2.1 %copy-start.18 = (f32[16,3,6,10,128]{4,0,1,3,2:T(8,128)S(1)}, f32[16,3,6,10,128]{4,0,1,3,2:T(8,128)}, u32[]{:S(2)}) copy-start(f32[16,3,6,10,128]{4,0,1,3,2:T(8,128)} %get-tuple-element.59) | copy-start | bytes 4423684
  57.8 2.5 %copy-start.19 = (f32[16,3,6,10,128]{4,0,1,3,2:T(8,128)S(1)}, f32[16,3,6,10,128]{4,0,1,3,2:T(8,128)}, u32[]{:S(2)}) copy-start(f32[16,3,6,10,128]{4,0,1,3,2:T(8,128)} %get-tuple-element.78) | copy-start | bytes 4423684
  60.4 1.7 %copy-start.2 = (f32[16,3,6,10,128]{4,0,1,3,2:T(8,128)S(1)}, f32[16,3,6,10,128]{4,0,1,3,2:T(8,128)}, u32[]{:S(2)}) copy-start(f32[16,3,6,10,128]{4,0,1,3,2:T(8,128)} %get-tuple-element.82) | copy-start | bytes 4423684
  60.4 2.2 %copy-start.3 = (f32[16,3,6,10,128]{4,0,1,3,2:T(8,128)S(1)}, f32[16,3,6,10,128]{4,0,1,3,2:T(8,128)}, u32[]{:S(2)}) copy-start(f32[16,3,6,10,128]{4,0,1,3,2:T(8,128)} %get-tuple-element.83) | copy-start | bytes 4423684
  62.5 2.1 %copy-start.1 = (f32[16,3,6,10,128]{4,0,1,3,2:T(8,128)S(1)}, f32[16,3,6,10,128]{4,0,1,3,2:T(8,128)}, u32[]{:S(2)}) copy-start(f32[16,3,6,10,128]{4,0,1,3,2:T(8,128)} %get-tuple-element.84) | copy-start | bytes 4423684
  62.5 10.4 %copy-start.33 = (f32[16,1,6,10,128]{4,0,1,3,2:T(8,128)S(1)}, f32[16,1,6,10,128]{4,0,1,3,2:T(8,128)}, u32[]{:S(2)}) copy-start(f32[16,1,6,10,128]{4,0,1,3,2:T(8,128)} %get-tuple-element.94) | copy-start | bytes 1474564
  62.5 10.4 %copy-start.34 = (f32[16,1,6,10,128]{4,0,1,3,2:T(8,128)S(1)}, f32[16,1,6,10,128]{4,0,1,3,2:T(8,128)}, u32[]{:S(2)}) copy-start(f32[16,1,6,10,128]{4,0,1,3,2:T(8,128)} %get-tuple-element.41) | copy-start | bytes 1474564
  62.5 10.4 %copy-start.35 = (f32[16,1,6,10,128]{4,0,1,3,2:T(8,128)S(1)}, f32[16,1,6,10,128]{4,0,1,3,2:T(8,128)}, u32[]{:S(2)}) copy-start(f32[16,1,6,10,128]{4,0,1,3,2:T(8,128)} %get-tuple-element.42) | copy-start | bytes 1474564
  62.6 10.4 %copy-start.36 = (f32[16,1,6,10,128]{4,0,1,3,2:T(8,128)S(1)}, f32[16,1,6,10,128]{4,0,1,3,2:T(8,128)}, u32[]{:S(2)}) copy-start(f32[16,1,6,10,128]{4,0,1,3,2:T(8,128)} %get-tuple-element.137) | copy-start | bytes 1474564
  62.6 10.4 %copy-start.37 = (f32[16,1,6,10,128]{4,0,1,3,2:T(8,128)S(1)}, f32[16,1,6,10,128]{4,0,1,3,2:T(8,128)}, u32[]{:S(2)}) copy-start(f32[16,1,6,10,128]{4,0,1,3,2:T(8,128)} %get-tuple-element.95) | copy-start | bytes 1474564
  62.6 10.4 %copy-start.38 = (f32[16,1,6,10,128]{4,0,1,3,2:T(8,128)S(1)}, f32[16,1,6,10,128]{4,0,1,3,2:T(8,128)}, u32[]{:S(2)}) copy-start(f32[16,1,6,10,128]{4,0,1,3,2:T(8,128)} %get-tuple-element.96) | copy-start | bytes 1474564
  64.6 8.4 %copy-start.23 = (f32[16,1,6,10,128]{4,0,1,3,2:T(8,128)S(1)}, f32[16,1,6,10,128]{4,0,1,3,2:T(8,128)}, u32[]{:S(2)}) copy-start(f32[16,1,6,10,128]{4,0,1,3,2:T(8,128)} %get-tuple-element.90) | copy-start | bytes 1474564
  64.6 8.4 %copy-start.24 = (f32[16,1,6,10,128]{4,0,1,3,2:T(8,128)S(1)}, f32[16,1,6,10,128]{4,0,1,3,2:T(8,128)}, u32[]{:S(2)}) copy-start(f32[16,1,6,10,128]{4,0,1,3,2:T(8,128)} %get-tuple-element.37) | copy-start | bytes 1474564
  64.6 8.4 %copy-start.25 = (f32[16,1,6,10,128]{4,0,1,3,2:T(8,128)S(1)}, f32[16,1,6,10,128]{4,0,1,3,2:T(8,128)}, u32[]{:S(2)}) copy-start(f32[16,1,6,10,128]{4,0,1,3,2:T(8,128)} %get-tuple-element.38) | copy-start | bytes 1474564
  64.6 8.4 %copy-start.26 = (f32[16,1,6,10,128]{4,0,1,3,2:T(8,128)S(1)}, f32[16,1,6,10,128]{4,0,1,3,2:T(8,128)}, u32[]{:S(2)}) copy-start(f32[16,1,6,10,128]{4,0,1,3,2:T(8,128)} %get-tuple-element.149) | copy-start | bytes 1474564
  64.6 8.4 %copy-start.27 = (f32[16,1,6,10,128]{4,0,1,3,2:T(8,128)S(1)}, f32[16,1,6,10,128]{4,0,1,3,2:T(8,128)}, u32[]{:S(2)}) copy-start(f32[16,1,6,10,128]{4,0,1,3,2:T(8,128)} %get-tuple-element.91) | copy-start | bytes 1474564
  64.6 8.4 %copy-start.28 = (f32[16,1,6,10,128]{4,0,1,3,2:T(8,128)S(1)}, f32[16,1,6,10,128]{4,0,1,3,2:T(8,128)}, u32[]{:S(2)}) copy-start(f32[16,1,6,10,128]{4,0,1,3,2:T(8,128)} %get-tuple-element.92) | copy-start | bytes 1474564
  64.7 8.4 %copy-start.29 = (f32[16,1,6,10,128]{4,0,1,3,2:T(8,128)S(1)}, f32[16,1,6,10,128]{4,0,1,3,2:T(8,128)}, u32[]{:S(2)}) copy-start(f32[16,1,6,10,128]{4,0,1,3,2:T(8,128)} %get-tuple-element.11) | copy-start | bytes 1474564
  64.7 8.4 %copy-start.30 = (f32[16,1,6,10,128]{4,0,1,3,2:T(8,128)S(1)}, f32[16,1,6,10,128]{4,0,1,3,2:T(8,128)}, u32[]{:S(2)}) copy-start(f32[16,1,6,10,128]{4,0,1,3,2:T(8,128)} %get-tuple-element.147) | copy-start | bytes 1474564
  64.7 8.4 %copy-start.31 = (f32[16,1,6,10,128]{4,0,1,3,2:T(8,128)S(1)}, f32[16,1,6,10,128]{4,0,1,3,2:T(8,128)}, u32[]{:S(2)}) copy-start(f32[16,1,6,10,128]{4,0,1,3,2:T(8,128)} %get-tuple-element.148) | copy-start | bytes 1474564
  64.7 8.4 %copy-start.32 = (f32[16,1,6,10,128]{4,0,1,3,2:T(8,128)S(1)}, f32[16,1,6,10,128]{4,0,1,3,2:T(8,128)}, u32[]{:S(2)}) copy-start(f32[16,1,6,10,128]{4,0,1,3,2:T(8,128)} %get-tuple-element.93) | copy-start | bytes 1474564
  66.1 7.0 %copy-start.20 = (f32[16,1,6,10,128]{4,0,1,3,2:T(8,128)S(1)}, f32[16,1,6,10,128]{4,0,1,3,2:T(8,128)}, u32[]{:S(2)}) copy-start(f32[16,1,6,10,128]{4,0,1,3,2:T(8,128)} %get-tuple-element.87) | copy-start | bytes 1474564
  66.1 7.0 %copy-start.21 = (f32[16,1,6,10,128]{4,0,1,3,2:T(8,128)S(1)}, f32[16,1,6,10,128]{4,0,1,3,2:T(8,128)}, u32[]{:S(2)}) copy-start(f32[16,1,6,10,128]{4,0,1,3,2:T(8,128)} %get-tuple-element.88) | copy-start | bytes 1474564
  66.1 7.0 %copy-start.22 = (f32[16,1,6,10,128]{4,0,1,3,2:T(8,128)S(1)}, f32[16,1,6,10,128]{4,0,1,3,2:T(8,128)}, u32[]{:S(2)}) copy-start(f32[16,1,6,10,128]{4,0,1,3,2:T(8,128)} %get-tuple-element.89) | copy-start | bytes 1474564
  66.2 2.9 %collective-permute-start.2 = (f32[6,1,128]{2,1,0:T(1,128)S(1)}, f32[6,1,128]{2,1,0:T(1,128)S(1)}, u32[]{:S(2)}, u32[]{:S(2)}) collective-permute-start(f32[6,1,128]{2,1,0:T(1,128)S(1)} %get-tuple-element.127), channel_id=1, source_target_pairs={{0,1},{1,2},{2,3},{3,4},{4,5},{5,6},{6,7},{8,9},{9,10},{10,11},{11... | collective-permute-start | bytes 9224 | tf_op jit(solution)/shard_map/ppermute | solution.py:21
  67.8 4.8 %collective-permute-start.3 = (f32[6,1,128]{2,1,0:T(1,128)S(1)}, f32[6,1,128]{2,1,0:T(1,128)S(1)}, u32[]{:S(2)}, u32[]{:S(2)}) collective-permute-start(f32[6,1,128]{2,1,0:T(1,128)S(1)} %get-tuple-element.128), channel_id=1, source_target_pairs={{1,0},{2,1},{3,2},{4,3},{5,4},{6,5},{7,6},{9,8},{10,9},{11,10},{12... | collective-permute-start | bytes 9224 | tf_op jit(solution)/shard_map/ppermute | solution.py:23
  89.4 1.1 copy-start
  93.4 7.2 %collective-permute-start.6 = (f32[16,3,6,1,128]{4,0,1,3,2:T(8,128)S(1)}, f32[16,3,6,1,128]{4,0,1,3,2:T(8,128)S(1)}, u32[]{:S(2)}, u32[]{:S(2)}) collective-permute-start(f32[16,3,6,1,128]{4,0,1,3,2:T(8,128)S(1)} %get-tuple-element.57), channel_id=1, source_target_pairs={{0,1},{1,2},{2,3},{3,4},{4,5},{5,6},{6,7},{8,9},{9,10},{10,11},{11... | collective-permute-start | bytes 442376 | tf_op jit(solution)/shard_map/ppermute | solution.py:21
  97.6 3.3 %collective-permute-start.7 = (f32[16,3,6,1,128]{4,0,1,3,2:T(8,128)S(1)}, f32[16,3,6,1,128]{4,0,1,3,2:T(8,128)S(1)}, u32[]{:S(2)}, u32[]{:S(2)}) collective-permute-start(f32[16,3,6,1,128]{4,0,1,3,2:T(8,128)S(1)} %get-tuple-element.58), channel_id=1, source_target_pairs={{1,0},{2,1},{3,2},{4,3},{5,4},{6,5},{7,6},{9,8},{10,9},{11,10},{12... | collective-permute-start | bytes 442376 | tf_op jit(solution)/shard_map/ppermute | solution.py:23
where the time goes:
time: 116 us; the launch traced here: 115 us
  other arithmetic  56.1 us (48%)
  starting transfers between devices  26.2 us (23%)
  local copies, waits for them, and re-layouts  12.3 us (11%)
  blocking collectives  12.3 us (11%)
  matrix products  4.34 us (4%)
  waiting for transfers between devices  3.65 us (3%)
    add x1, other arithmetic, apply_operator(): result = result + coupling * pushed  16.2 us
    ppermute x4, starting transfers between devices, extended(): lax.ppermute(head, axis, [((i + 1) % count, i) for i in range(ends)])  14.7 us
    sub x2, other arithmetic, apply_operator(): differ = centre - nearby  13.2 us
    all_to_all x1, blocking collectives, sum_at_owner(): lax.all_to_all(in_blocks(array, dim, peers), axis, 0, 0, tiled=True)  12.3 us
    ppermute x4, starting transfers between devices, extended(): lax.ppermute(tail, axis, [(i, (i + 1) % count) for i in range(ends)])  11.6 us
    unnamed x83, local copies, waits for them, and re-layouts  10.1 us
    mul x6, other arithmetic, apply_operator(): step_y * along_dir  9.02 us
    mul x6, other arithmetic, apply_operator(): beta_shear / reach_len  7.45 us
  transfers between devices with their start and end apart: 8, of which 2 were waited for; matrix products, arithmetic and copies ran while one was open for 53% of the time, Pallas kernels for 0%

commit v1 on v0

v1 whole, which is shorter than its diff:
```python
import functools
import jax
import jax.numpy as jnp
from jax import lax
from jax.experimental import pallas as pl
from jax.experimental.pallas import tpu as pltpu
from jax.sharding import PartitionSpec as P

GROUPS = 4
MODES = 16
CX = 4
CY = 8
NZ = 128

beta_shear = 0.5
mass_share = 0.1

Q1 = 0.5 * beta_shear
Q2 = 0.25 * beta_shear / 2
Q3 = 0.125 * beta_shear / 3
DIAG = 7.0 + 2 * Q1 + 8 * Q2 + 8 * Q3
HALF = 0.5 * (mass_share + DIAG)

KZ = {(0, 0): (0.0, 0.5), (0, 1): (0.5, 0.25), (1, 0): (0.5, 0.25), (1, 1): (0.25, 0.125)}


def diag_weights(comp, ax, ay):
    c, s = KZ[(ax, ay)]
    m = ax + ay
    if (comp == 0 and ax) or (comp == 1 and ay):
        c += (0.0, Q1, Q2)[m]
        s += (Q1, Q2, Q3)[m]
    if comp == 2:
        s += (Q1, Q2, Q3)[m]
    return c, s


def add(*terms):
    terms = [t for t in terms if t is not None]
    if not terms:
        return None
    total = terms[0]
    for t in terms[1:]:
        total = total + t
    return total


def sub(a, b):
    if b is None:
        return a
    if a is None:
        return -b
    return a - b


def mul(k, a):
    return None if a is None or k == 0.0 else k * a


def z_parts(v):
    lane = lax.broadcasted_iota(jnp.int32, v.shape, 1)
    up = jnp.where(lane < NZ - 1, pltpu.roll(v, NZ - 1, 1), 0.0)
    down = jnp.where(lane > 0, pltpu.roll(v, 1, 1), 0.0)
    return v, up + down, up - down


NONE3 = (None, None, None)


def line(minus, centre, plus, want0=True, want1=True):
    minus, centre, plus = [(NONE3,) * 3 if t is None else t for t in (minus, centre, plus)]
    sum_c = [add(plus[i][0], minus[i][0]) for i in range(3)]
    sum_s = [add(plus[i][1], minus[i][1]) for i in range(3)]
    diff_dz = sub(plus[2][2], minus[2][2])
    diff_dy = sub(plus[1][2], minus[1][2])
    same, even, odd = [None] * 3, [None] * 3, [None] * 3
    for i in range(3):
        parts = (centre[i][0], centre[i][1], sum_c[i], sum_s[i])
        if want0:
            k = diag_weights(i, 0, 0) + diag_weights(i, 0, 1)
            same[i] = add(*[mul(w, t) for w, t in zip(k, parts)])
        if want1:
            k = diag_weights(i, 1, 0) + diag_weights(i, 1, 1)
            even[i] = add(*[mul(w, t) for w, t in zip(k, parts)])
    if want0:
        same[1] = add(same[1], mul(Q2, diff_dz))
        same[2] = add(same[2], mul(Q2, diff_dy))
    if want1:
        even[1] = add(even[1], mul(Q3, diff_dz))
        even[2] = add(even[2], mul(Q3, diff_dy))
        diff = [add(mul(Q2, sub(plus[i][0], minus[i][0])), mul(Q3, sub(plus[i][1], minus[i][1]))) for i in (0, 1)]
        odd[1] = diff[0]
        odd[0] = add(diff[1], mul(Q2, centre[2][2]), mul(Q3, add(plus[2][2], minus[2][2])))
        odd[2] = add(mul(Q2, centre[0][2]), mul(Q3, add(plus[0][2], minus[0][2])))
    return same, even, odd


def scalar_line(minus, centre, plus):
    minus, centre, plus = [NONE3 if t is None else t for t in (minus, centre, plus)]
    sums = (centre[0], centre[1], add(plus[0], minus[0]), add(plus[1], minus[1]))
    same, even, odd = [None] * 6, [None] * 6, [None] * 6
    for i in range(3):
        same[i] = add(*[mul(w, t) for w, t in zip(diag_weights(i, 0, 0) + diag_weights(i, 0, 1), sums)])
        even[i] = add(*[mul(w, t) for w, t in zip(diag_weights(i, 1, 0) + diag_weights(i, 1, 1), sums)])
    diff_d = sub(plus[2], minus[2])
    same[5] = mul(Q2, diff_d)
    even[5] = mul(Q3, diff_d)
    odd[3] = add(mul(Q2, sub(plus[0], minus[0])), mul(Q3, sub(plus[1], minus[1])))
    odd[4] = add(mul(Q2, centre[2]), mul(Q3, add(plus[2], minus[2])))
    return same, even, odd


def times_g(g, v):
    return (
        g[0] * v[0] + g[3] * v[1] + g[4] * v[2],
        g[3] * v[0] + g[1] * v[1] + g[5] * v[2],
        g[4] * v[0] + g[5] * v[1] + g[2] * v[2],
    )


def put_split(ref, row, slot, value):
    high = value.astype(jnp.bfloat16)
    low = (value - high.astype(jnp.float32)).astype(jnp.bfloat16)
    lanes = pl.ds(slot * NZ, NZ)
    ref[pl.ds(row, MODES), lanes] = high
    ref[pl.ds(row + MODES, MODES), lanes] = low


def contract(a, b):
    return lax.dot_general(a, b, (((1,), (1,)), ((), ())), preferred_element_type=jnp.float32)


def fold(raw):
    return raw[:MODES] + raw[MODES:]


def shifted_rows(plane):
    row = lax.broadcasted_iota(jnp.int32, plane.shape, 0)
    plus = jnp.where(row < CY - 1, pltpu.roll(plane, CY - 1, 0), 0.0)
    minus = jnp.where(row > 0, pltpu.roll(plane, 1, 0), 0.0)
    return minus, plus


def own_kernel(z_ref, e_ref, q_ref, ux_ref, vx_ref, uy_ref, vy_ref, s_ref, d_ref, same_ref, lower_ref, upper_ref, g_ref, lhs_ref, rhs_ref):
    lines = []
    for x in range(CX):
        plane = e_ref[x]
        minus, plus = shifted_rows(plane)
        lines.append(scalar_line(z_parts(minus), z_parts(plane), z_parts(plus)))
    for x in range(CX):
        for n in range(6):
            total = lines[x][0][n]
            if x + 1 < CX:
                total = add(total, lines[x + 1][1][n], lines[x + 1][2][n])
            if x > 0:
                total = sub(add(total, lines[x - 1][1][n]), lines[x - 1][2][n])
            g_ref[x, n] = 0.5 * total

    for i in range(3):
        for y in range(CY + 1):
            zero = jnp.zeros((MODES, NZ), jnp.float32)
            lower_ref[CX, i, y] = zero
            upper_ref[0, i, y] = zero

    def spread(x, carry):
        for y in range(CY):
            for i in range(3):
                _, s, d = z_parts(z_ref[i, x, y])
                s_ref[x, i, y] = s
                d_ref[x, i, y] = d
        for y in range(CY + 1):
            cells = [
                tuple((z_ref[i, x, t], s_ref[x, i, t], d_ref[x, i, t]) for i in range(3)) if 0 <= t < CY else None
                for t in (y - 1, y, y + 1)
            ]
            same, even, odd = line(*cells)
            for i in range(3):
                same_ref[x, i, y] = same[i]
                lower_ref[x, i, y] = add(even[i], odd[i])
                upper_ref[x + 1, i, y] = sub(even[i], odd[i])
        return carry

    lax.fori_loop(0, CX, spread, 0)

    def gather(x, total):
        for y in range(CY):
            e = e_ref[x, pl.ds(y, 1), :]
            v = [z_ref[i, x, y] for i in range(3)]
            g = [g_ref[x, n, pl.ds(y, 1), :] for n in range(6)]
            gv = times_g(g, v)
            for i in range(3):
                u = same_ref[x, i, y] + lower_ref[x + 1, i, y] + upper_ref[x, i, y]
                put_split(lhs_ref, 0, y * 3 + i, e * (HALF * v[i] - u) + gv[i])
                put_split(rhs_ref, 0, y * 3 + i, v[i])
        for i in range(3):
            uy_ref[i, x] = same_ref[x, i, CY] + lower_ref[x + 1, i, CY] + upper_ref[x, i, CY]
        return total + contract(lhs_ref[...], rhs_ref[...])

    raw = lax.fori_loop(0, CX, gather, jnp.zeros((2 * MODES, 2 * MODES), jnp.float32))
    q_ref[...] = raw
    for i in range(3):
        for y in range(CY):
            ux_ref[i, y] = upper_ref[CX, i, y]

    def weighted(x, y):
        e = e_ref[x, pl.ds(y, 1), :]
        return tuple(z_parts(e * z_ref[i, x, y]) for i in range(3))

    rim = [weighted(CX - 1, y) for y in range(CY)]
    for y in range(CY):
        _, even, odd = line(rim[y - 1] if y > 0 else None, rim[y], rim[y + 1] if y + 1 < CY else None, want0=False)
        for i in range(3):
            vx_ref[i, y] = sub(even[i], odd[i])
    edge = [line(weighted(x, CY - 1), None, None) for x in range(CX)]
    for x in range(CX):
        for i in range(3):
            total = edge[x][0][i]
            if x + 1 < CX:
                total = add(total, edge[x + 1][1][i], edge[x + 1][2][i])
            if x > 0:
                total = sub(add(total, edge[x - 1][1][i]), edge[x - 1][2][i])
            vy_ref[i, x] = total


def corner_parts(cell, e_here, e_there, sy):
    def stencil(v):
        parts = tuple(z_parts(t) for t in v)
        _, even, odd = line(None, None, parts) if sy > 0 else line(parts, None, None)
        return [sub(even[i], odd[i]) for i in range(3)]
    u = stencil(cell)
    w = stencil([e_here * t for t in cell])
    return [-(e_there * a + b) for a, b in zip(u, w)]


def halo_kernel(near_ref, z_ref, e_ref, q_ref, ux_ref, vx_ref, uy_ref, vy_ref, x_ref, yp_ref, ym_ref, own_ref, msg_ref,
                g_ref, lx_ref, rx_ref, ly_ref, ry_ref, lm_ref, lr_ref, rr_ref):
    ex, eyp, eym = 3 * CY * MODES, 3 * CX * MODES, 3 * MODES
    zx = lambda i, y: x_ref[pl.ds((i * CY + y) * MODES, MODES), :]
    zyp = lambda i, x: yp_ref[pl.ds((i * CX + x) * MODES, MODES), :]
    zym = lambda i: ym_ref[pl.ds(i * MODES, MODES), :]
    row = lax.broadcasted_iota(jnp.int32, (CY, NZ), 0)

    lines = []
    for x in range(CX):
        plus = jnp.where(row == CY - 1, yp_ref[pl.ds(eyp + x, 1), :], 0.0)
        minus = jnp.where(row == 0, ym_ref[pl.ds(eym + x, 1), :], 0.0)
        lines.append((minus, plus))
    side = x_ref[pl.ds(ex, CY), :]
    minus, plus = shifted_rows(side)
    far = scalar_line(z_parts(minus), z_parts(side), z_parts(plus))
    halo = [scalar_line(z_parts(m), None, z_parts(p)) for m, p in lines]
    minus, plus = shifted_rows(e_ref[CX - 1])
    back = scalar_line(z_parts(minus + lines[CX - 1][0]), z_parts(e_ref[CX - 1]), z_parts(plus + lines[CX - 1][1]))
    for x in range(CX):
        after = far if x + 1 == CX else halo[x + 1]
        for n in range(6):
            total = add(halo[x][0][n], after[1][n], after[2][n])
            if x > 0:
                total = sub(add(total, halo[x - 1][1][n]), halo[x - 1][2][n])
            g_ref[x, n] = 0.5 * total
    for n in range(6):
        g_ref[CX, n] = sub(back[1][n], back[2][n])

    def g_at(x, y):
        return [g_ref[x, n, pl.ds(y, 1), :] for n in range(6)]

    columns = [(CX - 1, y) for y in range(CY)] + [(x, y) for x in range(CX - 1) for y in (0, CY - 1)]
    for slot, (x, y) in enumerate(columns):
        v = [z_ref[i, x, y] for i in range(3)]
        gv = times_g(g_at(x, y), v)
        for i in range(3):
            put_split(lr_ref, 0, slot * 3 + i, gv[i])
            put_split(rr_ref, 0, slot * 3 + i, v[i])

    for y in range(CY):
        v = [zx(i, y) for i in range(3)]
        gv = times_g(g_at(CX, y), v)
        e = x_ref[pl.ds(ex + y, 1), :]
        for i in range(3):
            put_split(lx_ref, 0, y * 3 + i, -(e * ux_ref[i, y] + vx_ref[i, y]))
            put_split(lx_ref, 2 * MODES, y * 3 + i, gv[i])
            put_split(rx_ref, 0, y * 3 + i, v[i])
    for x in range(CX):
        e = yp_ref[pl.ds(eyp + x, 1), :]
        for i in range(3):
            put_split(ly_ref, 0, x * 3 + i, -(e * uy_ref[i, x] + vy_ref[i, x]))
            put_split(ry_ref, 0, x * 3 + i, zyp(i, x))

    last = CX - 1
    up = [zyp(i, last) for i in range(3)]
    down = [zym(i) for i in range(3)]
    e_up, e_down = yp_ref[pl.ds(eyp + last, 1), :], ym_ref[pl.ds(eym + last, 1), :]
    e_top, e_low = x_ref[pl.ds(ex + CY - 1, 1), :], x_ref[pl.ds(ex, 1), :]
    d_up = corner_parts(up, e_up, e_top, 1)
    d_down = corner_parts(down, e_down, e_low, -1)

    def corner_g(e, sy):
        _, even, odd = scalar_line(*((z_parts(e), None, None) if sy > 0 else (None, None, z_parts(e))))
        return [0.5 * add(even[n], odd[n]) for n in range(6)]

    g_up = times_g(corner_g(e_top, 1), up)
    g_down = times_g(corner_g(e_low, -1), down)
    for i in range(3):
        put_split(lm_ref, 0, i, d_up[i])
        put_split(lm_ref, 2 * MODES, i, d_down[i])
        put_split(lm_ref, 4 * MODES, i, g_up[i])
        put_split(lm_ref, 6 * MODES, i, g_down[i])
        put_split(lm_ref, 8 * MODES, i, down[i])

    wide = 2 * MODES
    k3 = 3 * NZ
    low, top = slice(0, k3), slice((CY - 1) * k3, CY * k3)
    last_y = slice(last * k3, (last + 1) * k3)
    raw_self = q_ref[...] + contract(lr_ref[...], rr_ref[...])
    raw_x = contract(lx_ref[...], rx_ref[...])
    raw_y = contract(ly_ref[...], ry_ref[...])
    raw_up = contract(lm_ref[0:wide], rx_ref[:, top])
    raw_down = contract(lm_ref[wide:2 * wide], rx_ref[:, low])
    raw_gup = contract(lm_ref[2 * wide:3 * wide], ry_ref[:, last_y])
    raw_gdown = contract(lm_ref[3 * wide:4 * wide], lm_ref[4 * wide:5 * wide])
    blocks = [raw_self, raw_y, raw_gup, raw_gdown, raw_x[:wide], raw_up, raw_down, raw_x[wide:]]
    tall = jnp.concatenate([fold(t) for t in blocks], axis=0)
    rows = tall.shape[0]
    tall = jnp.concatenate([tall, jnp.zeros((rows, NZ - wide), jnp.float32)], axis=1)
    lane = lax.broadcasted_iota(jnp.int32, (rows, NZ), 1)
    tall = jnp.where(lane < MODES, tall + pltpu.roll(tall, NZ - MODES, 1), 0.0)
    for shift in (MODES, 2 * MODES, 4 * MODES):
        tall = tall + pltpu.roll(tall, shift, 1)
    here, above, below, ahead = near_ref[4], near_ref[5], near_ref[3], near_ref[7]
    group = lax.broadcasted_iota(jnp.int32, (MODES, NZ), 1) // MODES

    def placed(entries, g):
        total = jnp.zeros((MODES, NZ), jnp.float32)
        for n, r, c in entries:
            total = total + jnp.where(group == jnp.where(r == g, c, -1), tall[n * MODES:(n + 1) * MODES], 0.0)
        return total

    entries = [(0, here, here), (1, here, above), (2, above, above), (3, below, below)]
    entries += [(4, here, ahead + GROUPS), (5, above, ahead + GROUPS), (6, below, ahead + GROUPS)]
    wide_rows = jnp.concatenate([placed(entries, g) for g in range(GROUPS)], axis=0)
    side_rows = jnp.concatenate([placed([(7, ahead, ahead + GROUPS)], g) for g in range(GROUPS)], axis=0)
    half = GROUPS * MODES
    turned = jnp.concatenate([wide_rows, jnp.zeros_like(wide_rows)], axis=0).T
    lane = lax.broadcasted_iota(jnp.int32, (half, NZ), 1)
    both = pltpu.roll(wide_rows + turned[:half], half, 1)
    own_ref[:, 0:NZ] = jnp.where(lane >= half, both, 0.0)
    own_ref[:, NZ:NZ + half] = pltpu.roll(wide_rows, half, 1)[:, :half]
    msg_ref[...] = jnp.where(lane < half, turned[half:], side_rows)


def vmem(n):
    return [pl.BlockSpec(memory_space=pltpu.VMEM)] * n


def f32(*shape):
    return jax.ShapeDtypeStruct(shape, jnp.float32)


def shards(modes, region, stiffness, coarse_group):
    levels = jnp.arange(stiffness.shape[0], dtype=jnp.int32)
    e = jnp.sum(jnp.where(region[..., None] == levels, stiffness, 0.0), axis=-1)
    z = jnp.transpose(modes, (1, 2, 3, 0, 4))
    zeros = jnp.zeros((4, NZ), jnp.float32)
    pay_x = jnp.concatenate([z[:, 0].reshape(-1, NZ), e[0]], axis=0)
    pay_yp = jnp.concatenate([z[:, :, 0].reshape(-1, NZ), e[:, 0], zeros], axis=0)
    pay_ym = jnp.concatenate([z[:, CX - 1, CY - 1].reshape(-1, NZ), e[:, CY - 1], zeros], axis=0)
    n_gx, n_gy = lax.axis_size("gx"), lax.axis_size("gy")
    got_x = lax.ppermute(pay_x, "gx", [(i + 1, i) for i in range(n_gx - 1)])
    got_yp = lax.ppermute(pay_yp, "gy", [(i + 1, i) for i in range(n_gy - 1)])
    got_ym = lax.ppermute(pay_ym, "gy", [(i, i + 1) for i in range(n_gy - 1)])
    group_pad = jnp.pad(coarse_group, 1, constant_values=-1)
    near = lax.dynamic_slice(group_pad, (lax.axis_index("gx"), lax.axis_index("gy")), (3, 3)).reshape(9)

    col = (MODES, NZ)
    k_own, k_x, k_y, k_rim = 3 * CY * NZ, 3 * CY * NZ, 3 * CX * NZ, 42 * NZ
    wide = 2 * MODES
    bf16 = jnp.bfloat16
    q, ux, vx, uy, vy = pl.pallas_call(
        own_kernel,
        out_shape=[f32(wide, wide), f32(3, CY, *col), f32(3, CY, *col), f32(3, CX, *col), f32(3, CX, *col)],
        in_specs=vmem(2),
        out_specs=vmem(5),
        scratch_shapes=[
            pltpu.VMEM((CX, 3, CY, *col), jnp.float32),
            pltpu.VMEM((CX, 3, CY, *col), jnp.float32),
            pltpu.VMEM((CX, 3, CY + 1, *col), jnp.float32),
            pltpu.VMEM((CX + 1, 3, CY + 1, *col), jnp.float32),
            pltpu.VMEM((CX + 1, 3, CY + 1, *col), jnp.float32),
            pltpu.VMEM((CX, 6, CY, NZ), jnp.float32),
            pltpu.VMEM((wide, k_own), bf16),
            pltpu.VMEM((wide, k_own), bf16),
        ],
        cost_estimate=pl.CostEstimate(flops=4_000_000_000, bytes_accessed=1_000_000, transcendentals=0),
        name="own",
    )(z, e)
    own, msg = pl.pallas_call(
        halo_kernel,
        out_shape=[f32(GROUPS * MODES, 3 * GROUPS * MODES), f32(GROUPS * MODES, NZ)],
        in_specs=[pl.BlockSpec(memory_space=pltpu.SMEM)] + vmem(10),
        out_specs=vmem(2),
        scratch_shapes=[
            pltpu.VMEM((CX + 1, 6, CY, NZ), jnp.float32),
            pltpu.VMEM((2 * wide, k_x), bf16),
            pltpu.VMEM((wide, k_x), bf16),
            pltpu.VMEM((wide, k_y), bf16),
            pltpu.VMEM((wide, k_y), bf16),
            pltpu.VMEM((5 * wide, 3 * NZ), bf16),
            pltpu.VMEM((wide, k_rim), bf16),
            pltpu.VMEM((wide, k_rim), bf16),
        ],
        cost_estimate=pl.CostEstimate(flops=500_000_000, bytes_accessed=500_000, transcendentals=0),
        name="halo",
    )(near, z, e, q, ux, vx, uy, vy, got_x, got_yp, got_ym)
    got = lax.ppermute(msg, "gx", [(i, i + 1) for i in range(n_gx - 1)])
    rows = own + jnp.pad(got, ((0, 0), (0, own.shape[1] - NZ)))
    parts = lax.all_to_all(rows.reshape(n_gy, -1, own.shape[1]), "gy", 0, 0, tiled=True)
    return jnp.sum(parts, axis=0)[None]


def solution(mesh):
    in_specs = (P(None, None, "gx", "gy", None), P("gx", "gy", None), P(), P())
    out_specs = P("gx", "gy", None)
    return jax.shard_map(shards, mesh=mesh, in_specs=in_specs, out_specs=out_specs, check_vma=False)
```

time: 116 us -> 46.1 us (0.40)
  other arithmetic: 56.1 us -> 2.35 us
  starting transfers between devices: 26.2 us -> 12.9 us
  local copies, waits for them, and re-layouts: 12.3 us -> 3.78 us
  Pallas kernels: 0 us -> 8.08 us
  matrix products: 4.34 us -> 0 us
  waiting for transfers between devices: 3.65 us -> 6.21 us
    mul x21 -> x0, other arithmetic: 23.7 us -> none  [the longest x6 9.02 us: apply_operator(): step_y * along_dir]
    add x1 -> x0, other arithmetic: 16.2 us -> none  [apply_operator(): result = result + coupling * pushed]
    ppermute x8 -> x4, starting transfers between devices: 26.2 us -> 12.9 us  [the longest x1 7.94 us: shards(): got_x = lax.ppermute(pay_x, 'gx', [(i + 1, i) for i in range(n_gx - 1)])]
    sub x2 -> x0, other arithmetic: 13.2 us -> none  [apply_operator(): differ = centre - nearby]
    pallas_call x0 -> x2, Pallas kernels: none -> 8.08 us  [the longest x1 4.67 us: shards(): pl.pallas_call(own_kernel, out_shape=[f32(wide, wide), f32(3, CY, *col),...]
    unnamed x83 -> x13, local copies, waits for them, and re-layouts: 10.1 us -> 2.97 us
    dot_general x10 -> x0, matrix products: 4.34 us -> none  [the longest x9 4.05 us: contract(): jnp.einsum('kaxyz,jaxyz->kj', left_side, right_side, precision=lax.Precis...]
    ppermute x8 -> x4, waiting for transfers between devices: 3.65 us -> 6.21 us  [the longest x1 6.2 us: shards(): got = lax.ppermute(msg, 'gx', [(i, i + 1) for i in range(n_gx - 1)])]
  transfers between devices with their start and end apart: 8 -> 4, of which waited for: 2 -> 1; matrix products, arithmetic and copies ran while one was open for 53% -> 2% of each run, Pallas kernels for 0% -> 10%
where the time goes in v1:
time: 46.1 us; the launch traced here: 45.7 us
  starting transfers between devices  12.9 us (28%)
  blocking collectives  12.2 us (26%)
  Pallas kernels  8.08 us (18%)
  waiting for transfers between devices  6.21 us (13%)
  local copies, waits for them, and re-layouts  3.78 us (8%)
  other arithmetic  2.35 us (5%)
    all_to_all x1, blocking collectives, shards(): lax.all_to_all(rows.reshape(n_gy, -1, own.shape[1]), 'gy', 0, 0, tiled=True)  12.2 us
    ppermute x1, starting transfers between devices, shards(): got_x = lax.ppermute(pay_x, 'gx', [(i + 1, i) for i in range(n_gx - 1)])  7.94 us
    ppermute x1, waiting for transfers between devices, shards(): got = lax.ppermute(msg, 'gx', [(i, i + 1) for i in range(n_gx - 1)])  6.2 us
    pallas_call x1, Pallas kernels, shards(): pl.pallas_call(own_kernel, out_shape=[f32(wide, wide), f32(3, CY, *col),...  4.67 us
    pallas_call x1, Pallas kernels, shards(): pl.pallas_call(halo_kernel, out_shape=[f32(GROUPS * MODES, 3 * GROUPS * M...  3.4 us
    unnamed x13, local copies, waits for them, and re-layouts  2.97 us
    ppermute x1, starting transfers between devices, shards(): got = lax.ppermute(msg, 'gx', [(i, i + 1) for i in range(n_gx - 1)])  1.91 us
    ppermute x1, starting transfers between devices, shards(): got_ym = lax.ppermute(pay_ym, 'gy', [(i, i + 1) for i in range(n_gy - 1)])  1.74 us
  transfers between devices with their start and end apart: 4, of which 1 were waited for; matrix products, arithmetic and copies ran while one was open for 2% of the time, Pallas kernels for 10%

profile of v1, /device:TPU:24, one launch (start us, length us, event | category | flops | bytes accessed | tf_op | source)
XLA Modules:
  0.0 45.7 jit_solution(17870688390720818956)
XLA Ops:
  0.0 0.9 %select_reduce_fusion.e_ref = f32[4,8,128]{2,1,0:T(8,128)S(1)} fusion(f32[16]{0:T(128)} %param.6, s32[4,8,128]{2,1,0:T(8,128)} %param.5), kind=kLoop, calls=%fused_computation.1 | loop fusion | flops 192512 | bytes 32832 | tf_op jit(solution)/shard_map/reduce_sum | solution.py:361
  0.9 0.0 copy-start.1
  0.9 1.6 %copy.16 = f32[16,3,4,8,128]{4,0,3,2,1:T(8,128)S(1)} copy(f32[16,3,4,8,128]{4,3,2,1,0:T(8,128)} %param.4) | data formatting | bytes 1572864 | tf_op args[0]
  2.5 0.0 copy-start
  2.5 1.7 %collective-permute-start.2 = (f32[56,128]{1,0:T(8,128)S(1)}, f32[56,128]{1,0:T(8,128)S(1)}, u32[]{:S(2)}, u32[]{:S(2)}) collective-permute-start(f32[56,128]{1,0:T(8,128)S(1)} %pad_maximum_fusion.2), channel_id=1, source_target_pairs={{0,1},{1,2},{2,3},{3,4},{4,5},{5,6},{6,7},{8,9},{9,10},{10,11},{11... | collective-permute-start | bytes 86024 | tf_op jit(solution)/shard_map/ppermute | solution.py:370
  4.3 1.3 %collective-permute-start.1 = (f32[200,128]{1,0:T(8,128)S(1)}, f32[200,128]{1,0:T(8,128)S(1)}, u32[]{:S(2)}, u32[]{:S(2)}) collective-permute-start(f32[200,128]{1,0:T(8,128)S(1)} %pad_maximum_fusion.1), channel_id=1, source_target_pairs={{1,0},{2,1},{3,2},{4,3},{5,4},{6,5},{7,6},{9,8},{10,9},{11,10},{12... | collective-permute-start | bytes 307208 | tf_op jit(solution)/shard_map/ppermute | solution.py:369
  5.6 0.0 copy-done.1
  5.7 7.9 %collective-permute-start = (f32[392,128]{1,0:T(8,128)S(1)}, f32[392,128]{1,0:T(8,128)S(1)}, u32[]{:S(2)}, u32[]{:S(2)}) collective-permute-start(f32[392,128]{1,0:T(8,128)S(1)} %pad_maximum_fusion), channel_id=1, source_target_pairs={{8,0},{16,8},{24,16},{32,24},{40,32},{48,40},{56,48},{64,56},{72,6... | collective-permute-start | bytes 602120 | tf_op jit(solution)/shard_map/ppermute | solution.py:368
  13.6 0.0 copy-done
  13.6 4.7 %own.1 = (f32[32,32]{1,0:T(8,128)}, f32[3,8,16,128]{3,2,1,0:T(8,128)}, f32[3,8,16,128]{3,2,1,0:T(8,128)}, f32[3,4,16,128]{3,2,1,0:T(8,128)}, f32[3,4,16,128]{3,2,1,0:T(8,128)}) custom-call(f32[3,4,8,16,128]{4,3,2,1,0:T(8,128)} %bitcast.20, f32[4,8,128]{2,1,0:T(8,128)} %copy-done.1), custom_call_target="tpu_custom_call" | custom-call | flops 4000000000 | bytes 1000000 | tf_op jit(solution)/shard_map/own/pallas_call | solution.py:378
  18.3 0.0 copy-start.2
  18.3 0.7 %copy-done.2 = s32[32,8]{0,1:T(8,128)S(1)} copy-done((s32[32,8]{0,1:T(8,128)S(1)}, s32[32,8]{0,1:T(8,128)}, u32[]{:S(2)}) %copy-start.2) | copy-done | bytes 1048
  19.0 0.1 pad_dynamic-slice_fusion
  19.1 0.1 copy.9
  19.2 0.6 %reshape.7.near_ref = s32[9]{0:T(128)} reshape(s32[3,3]{1,0:T(4,128)S(1)} %copy.9) | data formatting | bytes 72 | tf_op jit(solution)/shard_map/reshape | solution.py:372
  19.8 0.0 collective-permute-done.2.ym_ref
  19.8 0.0 copy-start.5
  19.8 0.0 collective-permute-done.1.yp_ref
  19.8 0.0 copy-start.4
  19.8 0.0 collective-permute-done.x_ref
  19.8 0.0 copy-start.3
  19.8 0.6 %copy-done.5 = f32[56,128]{1,0:T(8,128)} copy-done((f32[56,128]{1,0:T(8,128)}, f32[56,128]{1,0:T(8,128)S(1)}, u32[]{:S(2)}) %copy-start.5) | copy-done | bytes 28696
  20.4 0.0 copy-done.4
  20.4 0.1 copy-done.3
  20.5 3.4 %halo.1 = (f32[64,192]{1,0:T(8,128)}, f32[64,128]{1,0:T(8,128)}) custom-call(s32[9]{0:T(128)} %reshape.7.near_ref, f32[3,4,8,16,128]{4,3,2,1,0:T(8,128)} %bitcast.21, f32[4,8,128]{2,1,0:T(8,128)} %copy-done.1, f32[32,32]{1,0:T(8,128)} %get-tuple-element.12.q_ref, f32[3,8,16,128]{3,2,1,0:T(8,128)} %get-tuple-element.13.ux_ref, ...), custom_call_target="tpu_custom_call" | custom-call | flops 500000000 | bytes 500000 | tf_op jit(solution)/shard_map/halo/pallas_call | solution.py:396
  23.9 1.9 %collective-permute-start.3 = (f32[64,128]{1,0:T(8,128)}, f32[64,128]{1,0:T(8,128)S(1)}, u32[]{:S(2)}, u32[]{:S(2)}) collective-permute-start(f32[64,128]{1,0:T(8,128)} %get-tuple-element.18), channel_id=1, source_target_pairs={{0,8},{8,16},{16,24},{24,32},{32,40},{40,48},{48,56},{56,64},{64,7... | collective-permute-start | bytes 98312 | tf_op jit(solution)/shard_map/ppermute | solution.py:414
  25.8 6.2 %collective-permute-done.3 = f32[64,128]{1,0:T(8,128)S(1)} collective-permute-done((f32[64,128]{1,0:T(8,128)}, f32[64,128]{1,0:T(8,128)S(1)}, u32[]{:S(2)}, u32[]{:S(2)}) %collective-permute-start.3) | collective-permute-done | bytes 32800 | tf_op jit(solution)/shard_map/ppermute | solution.py:414
  32.0 0.8 %add_bitcast_fusion = f32[8,8,192]{2,1,0:T(8,128)S(1)} fusion(f32[64,192]{1,0:T(8,128)} %get-tuple-element.17, f32[64,128]{1,0:T(8,128)S(1)} %collective-permute-done.3), kind=kLoop, calls=%fused_computation.5 | loop fusion | flops 12288 | bytes 131072 | tf_op jit(solution)/shard_map/reshape | solution.py:416
  32.9 12.2 %all_to_all.5 = f32[8,8,192]{2,1,0:T(8,128)S(1)} all-to-all(f32[8,8,192]{2,1,0:T(8,128)S(1)} %add_bitcast_fusion), channel_id=1, replica_groups=mesh['gx'=32,'gy'=8] {'gy'}, dimensions={0} | all-to-all | bytes 98304 | tf_op jit(solution)/shard_map/all_to_all | solution.py:416
  45.1 0.6 %reduce_sum.19 = f32[8,192]{1,0:T(8,128)} reduce(f32[8,8,192]{2,1,0:T(8,128)S(1)} %all_to_all.5, f32[]{:T(128)} %constant.20.clone.1), dimensions={0}, to_apply=%region_1.2 | reduce | flops 10752 | bytes 55300 | tf_op jit(solution)/shard_map/reduce_sum | solution.py:417
  (9 shorter events, 0.1 us)
Async XLA Ops:
  0.9 4.8 %copy-start.1 = (f32[4,8,128]{2,1,0:T(8,128)}, f32[4,8,128]{2,1,0:T(8,128)S(1)}, u32[]{:S(2)}) copy-start(f32[4,8,128]{2,1,0:T(8,128)S(1)} %select_reduce_fusion.e_ref) | copy-start | bytes 49156
  2.5 11.2 %copy-start = (f32[16,3,4,8,128]{4,0,3,2,1:T(8,128)}, f32[16,3,4,8,128]{4,0,3,2,1:T(8,128)S(1)}, u32[]{:S(2)}) copy-start(f32[16,3,4,8,128]{4,0,3,2,1:T(8,128)S(1)} %copy.16) | copy-start | bytes 2359300
  2.5 17.2 %collective-permute-start.2 = (f32[56,128]{1,0:T(8,128)S(1)}, f32[56,128]{1,0:T(8,128)S(1)}, u32[]{:S(2)}, u32[]{:S(2)}) collective-permute-start(f32[56,128]{1,0:T(8,128)S(1)} %pad_maximum_fusion.2), channel_id=1, source_target_pairs={{0,1},{1,2},{2,3},{3,4},{4,5},{5,6},{6,7},{8,9},{9,10},{10,11},{11... | collective-permute-start | bytes 86024 | tf_op jit(solution)/shard_map/ppermute | solution.py:370
  4.3 15.5 %collective-permute-start.1 = (f32[200,128]{1,0:T(8,128)S(1)}, f32[200,128]{1,0:T(8,128)S(1)}, u32[]{:S(2)}, u32[]{:S(2)}) collective-permute-start(f32[200,128]{1,0:T(8,128)S(1)} %pad_maximum_fusion.1), channel_id=1, source_target_pairs={{1,0},{2,1},{3,2},{4,3},{5,4},{6,5},{7,6},{9,8},{10,9},{11,10},{12... | collective-permute-start | bytes 307208 | tf_op jit(solution)/shard_map/ppermute | solution.py:369
  5.7 14.1 %collective-permute-start = (f32[392,128]{1,0:T(8,128)S(1)}, f32[392,128]{1,0:T(8,128)S(1)}, u32[]{:S(2)}, u32[]{:S(2)}) collective-permute-start(f32[392,128]{1,0:T(8,128)S(1)} %pad_maximum_fusion), channel_id=1, source_target_pairs={{8,0},{16,8},{24,16},{32,24},{40,32},{48,40},{56,48},{64,56},{72,6... | collective-permute-start | bytes 602120 | tf_op jit(solution)/shard_map/ppermute | solution.py:368
  18.3 0.7 %copy-start.2 = (s32[32,8]{0,1:T(8,128)S(1)}, s32[32,8]{0,1:T(8,128)}, u32[]{:S(2)}) copy-start(s32[32,8]{0,1:T(8,128)} %param.7) | copy-start | bytes 3076
  19.8 0.6 %copy-start.5 = (f32[56,128]{1,0:T(8,128)}, f32[56,128]{1,0:T(8,128)S(1)}, u32[]{:S(2)}) copy-start(f32[56,128]{1,0:T(8,128)S(1)} %collective-permute-done.2.ym_ref) | copy-start | bytes 86020
  19.8 0.6 %copy-start.4 = (f32[200,128]{1,0:T(8,128)}, f32[200,128]{1,0:T(8,128)S(1)}, u32[]{:S(2)}) copy-start(f32[200,128]{1,0:T(8,128)S(1)} %collective-permute-done.1.yp_ref) | copy-start | bytes 307204
  19.8 0.7 %copy-start.3 = (f32[392,128]{1,0:T(8,128)}, f32[392,128]{1,0:T(8,128)S(1)}, u32[]{:S(2)}) copy-start(f32[392,128]{1,0:T(8,128)S(1)} %collective-permute-done.x_ref) | copy-start | bytes 602116
  23.9 8.1 %collective-permute-start.3 = (f32[64,128]{1,0:T(8,128)}, f32[64,128]{1,0:T(8,128)S(1)}, u32[]{:S(2)}, u32[]{:S(2)}) collective-permute-start(f32[64,128]{1,0:T(8,128)} %get-tuple-element.18), channel_id=1, source_target_pairs={{0,8},{8,16},{16,24},{24,32},{32,40},{40,48},{48,56},{56,64},{64,7... | collective-permute-start | bytes 98312 | tf_op jit(solution)/shard_map/ppermute | solution.py:414

commit v2 on v1

v2 whole, which is shorter than its diff:
```python
import jax
import jax.numpy as jnp
from jax import lax
from jax.experimental import pallas as pl
from jax.experimental.pallas import tpu as pltpu
from jax.sharding import PartitionSpec as P

GROUPS = 4
MODES = 16
CX = 4
CY = 8
NZ = 128

beta_shear = 0.5
mass_share = 0.1

Q1 = 0.5 * beta_shear
Q2 = 0.25 * beta_shear / 2
Q3 = 0.125 * beta_shear / 3
DIAG = 7.0 + 2 * Q1 + 8 * Q2 + 8 * Q3
HALF = 0.5 * (mass_share + DIAG)

KZ = {(0, 0): (0.0, 0.5), (0, 1): (0.5, 0.25), (1, 0): (0.5, 0.25), (1, 1): (0.25, 0.125)}


def diag_weights(comp, ax, ay):
    c, s = KZ[(ax, ay)]
    m = ax + ay
    if (comp == 0 and ax) or (comp == 1 and ay):
        c += (0.0, Q1, Q2)[m]
        s += (Q1, Q2, Q3)[m]
    if comp == 2:
        s += (Q1, Q2, Q3)[m]
    return c, s


def add(*terms):
    terms = [t for t in terms if t is not None]
    if not terms:
        return None
    total = terms[0]
    for t in terms[1:]:
        total = total + t
    return total


def sub(a, b):
    if b is None:
        return a
    if a is None:
        return -b
    return a - b


def mul(k, a):
    return None if a is None or k == 0.0 else k * a


def z_parts(v):
    lane = lax.broadcasted_iota(jnp.int32, v.shape, 1)
    up = jnp.where(lane < NZ - 1, pltpu.roll(v, NZ - 1, 1), 0.0)
    down = jnp.where(lane > 0, pltpu.roll(v, 1, 1), 0.0)
    return v, up + down, up - down


NONE3 = (None, None, None)


def line(minus, centre, plus, want0=True, want1=True):
    minus, centre, plus = [(NONE3,) * 3 if t is None else t for t in (minus, centre, plus)]
    sum_c = [add(plus[i][0], minus[i][0]) for i in range(3)]
    sum_s = [add(plus[i][1], minus[i][1]) for i in range(3)]
    diff_dz = sub(plus[2][2], minus[2][2])
    diff_dy = sub(plus[1][2], minus[1][2])
    same, even, odd = [None] * 3, [None] * 3, [None] * 3
    for i in range(3):
        parts = (centre[i][0], centre[i][1], sum_c[i], sum_s[i])
        if want0:
            k = diag_weights(i, 0, 0) + diag_weights(i, 0, 1)
            same[i] = add(*[mul(w, t) for w, t in zip(k, parts)])
        if want1:
            k = diag_weights(i, 1, 0) + diag_weights(i, 1, 1)
            even[i] = add(*[mul(w, t) for w, t in zip(k, parts)])
    if want0:
        same[1] = add(same[1], mul(Q2, diff_dz))
        same[2] = add(same[2], mul(Q2, diff_dy))
    if want1:
        even[1] = add(even[1], mul(Q3, diff_dz))
        even[2] = add(even[2], mul(Q3, diff_dy))
        diff = [add(mul(Q2, sub(plus[i][0], minus[i][0])), mul(Q3, sub(plus[i][1], minus[i][1]))) for i in (0, 1)]
        odd[1] = diff[0]
        odd[0] = add(diff[1], mul(Q2, centre[2][2]), mul(Q3, add(plus[2][2], minus[2][2])))
        odd[2] = add(mul(Q2, centre[0][2]), mul(Q3, add(plus[0][2], minus[0][2])))
    return same, even, odd


def scalar_line(minus, centre, plus):
    minus, centre, plus = [NONE3 if t is None else t for t in (minus, centre, plus)]
    sums = (centre[0], centre[1], add(plus[0], minus[0]), add(plus[1], minus[1]))
    same, even, odd = [None] * 6, [None] * 6, [None] * 6
    for i in range(3):
        same[i] = add(*[mul(w, t) for w, t in zip(diag_weights(i, 0, 0) + diag_weights(i, 0, 1), sums)])
        even[i] = add(*[mul(w, t) for w, t in zip(diag_weights(i, 1, 0) + diag_weights(i, 1, 1), sums)])
    diff_d = sub(plus[2], minus[2])
    same[5] = mul(Q2, diff_d)
    even[5] = mul(Q3, diff_d)
    odd[3] = add(mul(Q2, sub(plus[0], minus[0])), mul(Q3, sub(plus[1], minus[1])))
    odd[4] = add(mul(Q2, centre[2]), mul(Q3, add(plus[2], minus[2])))
    return same, even, odd


def times_g(g, v):
    return (
        g[0] * v[0] + g[3] * v[1] + g[4] * v[2],
        g[3] * v[0] + g[1] * v[1] + g[5] * v[2],
        g[4] * v[0] + g[5] * v[1] + g[2] * v[2],
    )


def put_split(ref, row, slot, value):
    high = value.astype(jnp.bfloat16)
    low = (value - high.astype(jnp.float32)).astype(jnp.bfloat16)
    lanes = pl.ds(slot * NZ, NZ)
    ref[pl.ds(row, MODES), lanes] = high
    ref[pl.ds(row + MODES, MODES), lanes] = low


def contract(a, b):
    return lax.dot_general(a, b, (((1,), (1,)), ((), ())), preferred_element_type=jnp.float32)


def fold(raw):
    return raw[:MODES] + raw[MODES:]


def shifted_rows(plane):
    row = lax.broadcasted_iota(jnp.int32, plane.shape, 0)
    plus = jnp.where(row < CY - 1, pltpu.roll(plane, CY - 1, 0), 0.0)
    minus = jnp.where(row > 0, pltpu.roll(plane, 1, 0), 0.0)
    return minus, plus


def own_kernel(z_ref, e_ref, q_ref, ux_ref, vx_ref, uy_ref, vy_ref, s_ref, d_ref, same_ref, lower_ref, upper_ref, g_ref, lhs_ref, rhs_ref):
    lines = []
    for x in range(CX):
        plane = e_ref[x]
        minus, plus = shifted_rows(plane)
        lines.append(scalar_line(z_parts(minus), z_parts(plane), z_parts(plus)))
    for x in range(CX):
        for n in range(6):
            total = lines[x][0][n]
            if x + 1 < CX:
                total = add(total, lines[x + 1][1][n], lines[x + 1][2][n])
            if x > 0:
                total = sub(add(total, lines[x - 1][1][n]), lines[x - 1][2][n])
            g_ref[x, n] = 0.5 * total

    for i in range(3):
        for y in range(CY + 1):
            zero = jnp.zeros((MODES, NZ), jnp.float32)
            lower_ref[CX, i, y] = zero
            upper_ref[0, i, y] = zero

    def spread(x, carry):
        for y in range(CY):
            for i in range(3):
                _, s, d = z_parts(z_ref[i, x, y])
                s_ref[x, i, y] = s
                d_ref[x, i, y] = d
        for y in range(CY + 1):
            cells = [
                tuple((z_ref[i, x, t], s_ref[x, i, t], d_ref[x, i, t]) for i in range(3)) if 0 <= t < CY else None
                for t in (y - 1, y, y + 1)
            ]
            same, even, odd = line(*cells)
            for i in range(3):
                same_ref[x, i, y] = same[i]
                lower_ref[x, i, y] = add(even[i], odd[i])
                upper_ref[x + 1, i, y] = sub(even[i], odd[i])
        return carry

    lax.fori_loop(0, CX, spread, 0)

    def gather(x, total):
        for y in range(CY):
            e = e_ref[x, pl.ds(y, 1), :]
            v = [z_ref[i, x, y] for i in range(3)]
            g = [g_ref[x, n, pl.ds(y, 1), :] for n in range(6)]
            gv = times_g(g, v)
            for i in range(3):
                u = same_ref[x, i, y] + lower_ref[x + 1, i, y] + upper_ref[x, i, y]
                put_split(lhs_ref, 0, y * 3 + i, e * (HALF * v[i] - u) + gv[i])
                put_split(rhs_ref, 0, y * 3 + i, v[i])
        for i in range(3):
            uy_ref[i, x] = same_ref[x, i, CY] + lower_ref[x + 1, i, CY] + upper_ref[x, i, CY]
        return total + contract(lhs_ref[...], rhs_ref[...])

    raw = lax.fori_loop(0, CX, gather, jnp.zeros((2 * MODES, 2 * MODES), jnp.float32))
    q_ref[...] = raw
    for i in range(3):
        for y in range(CY):
            ux_ref[0, i, y] = upper_ref[CX, i, y]
            ux_ref[1, i, y] = lower_ref[0, i, y]

    def weighted(x, y):
        e = e_ref[x, pl.ds(y, 1), :]
        return tuple(z_parts(e * z_ref[i, x, y]) for i in range(3))

    for side, x in enumerate((CX - 1, 0)):
        rim = [weighted(x, y) for y in range(CY)]
        for y in range(CY):
            _, even, odd = line(rim[y - 1] if y > 0 else None, rim[y], rim[y + 1] if y + 1 < CY else None, want0=False)
            for i in range(3):
                vx_ref[side, i, y] = (add, sub)[side == 0](even[i], odd[i])
    edge = [line(weighted(x, CY - 1), None, None) for x in range(CX)]
    for x in range(CX):
        for i in range(3):
            total = edge[x][0][i]
            if x + 1 < CX:
                total = add(total, edge[x + 1][1][i], edge[x + 1][2][i])
            if x > 0:
                total = sub(add(total, edge[x - 1][1][i]), edge[x - 1][2][i])
            vy_ref[i, x] = total


SIDES = (0, 1)
EDGE = (CX - 1, 0)


def y_kernel(z_ref, e_ref, q_ref, uy_ref, vy_ref, yp_ref, ym_ref, raw_ref, cu_ref, cv_ref, cz_ref,
             g_ref, ly_ref, ry_ref, lr_ref, rr_ref):
    eyp, eym = 3 * CX * MODES, 6 * MODES
    row = lax.broadcasted_iota(jnp.int32, (CY, NZ), 0)
    halo = []
    for x in range(CX):
        plus = jnp.where(row == CY - 1, yp_ref[pl.ds(eyp + x, 1), :], 0.0)
        minus = jnp.where(row == 0, ym_ref[pl.ds(eym + x, 1), :], 0.0)
        halo.append(scalar_line(z_parts(minus), None, z_parts(plus)))
    for x in range(CX):
        for n in range(6):
            total = halo[x][0][n]
            if x + 1 < CX:
                total = add(total, halo[x + 1][1][n], halo[x + 1][2][n])
            if x > 0:
                total = sub(add(total, halo[x - 1][1][n]), halo[x - 1][2][n])
            g_ref[x, n] = 0.5 * total
    for slot, (x, y) in enumerate([(x, y) for x in range(CX) for y in (0, CY - 1)]):
        v = [z_ref[i, x, y] for i in range(3)]
        gv = times_g([g_ref[x, n, pl.ds(y, 1), :] for n in range(6)], v)
        for i in range(3):
            put_split(lr_ref, 0, slot * 3 + i, gv[i])
            put_split(rr_ref, 0, slot * 3 + i, v[i])
    for x in range(CX):
        e = yp_ref[pl.ds(eyp + x, 1), :]
        for i in range(3):
            put_split(ly_ref, 0, x * 3 + i, -(e * uy_ref[i, x] + vy_ref[i, x]))
            put_split(ry_ref, 0, x * 3 + i, yp_ref[pl.ds((i * CX + x) * MODES, MODES), :])
    raw_ref[0] = q_ref[...] + contract(lr_ref[...], rr_ref[...])
    raw_ref[1] = contract(ly_ref[...], ry_ref[...])
    for side in SIDES:
        x = EDGE[side]
        for n, sy in enumerate((1, -1)):
            if sy > 0:
                v = [yp_ref[pl.ds((i * CX + x) * MODES, MODES), :] for i in range(3)]
                e = yp_ref[pl.ds(eyp + x, 1), :]
            else:
                v = [ym_ref[pl.ds((side * 3 + i) * MODES, MODES), :] for i in range(3)]
                e = ym_ref[pl.ds(eym + x, 1), :]
            for out_ref, field in ((cu_ref, v), (cv_ref, [e * t for t in v])):
                parts = tuple(z_parts(t) for t in field)
                _, even, odd = line(None, None, parts, want0=False) if sy > 0 else line(parts, None, None, want0=False)
                for i in range(3):
                    out_ref[side, n, i] = (add, sub)[side == 0](even[i], odd[i])
            for i in range(3):
                put_split(cz_ref, (n * 2) * MODES, side * 3 + i, v[i])


def x_kernel(cg_ref, z_ref, raw_ref, ux_ref, vx_ref, cu_ref, cv_ref, cz_ref, first_ref, second_ref, out_ref,
             g_ref, lx_ref, rx_ref, lc_ref, lg_ref, lr_ref, rr_ref):
    a, b = lax.axis_index("gx"), lax.axis_index("gy")
    even_strip = a % 2 == 0
    wide = 2 * MODES

    def face(side, at):
        here, there = (first_ref[at, :], second_ref[at, :]) if side == 0 else (second_ref[at, :], first_ref[at, :])
        return jnp.where(even_strip, here, there)

    for slot, (side, y) in enumerate([(side, y) for side in SIDES for y in range(CY)]):
        for i in range(3):
            put_split(rr_ref, 0, slot * 3 + i, z_ref[i, EDGE[side], y])
    ex = 3 * CY * MODES
    for side in SIDES:
        plane = face(side, pl.ds(ex, CY))
        minus, plus = shifted_rows(plane)
        _, even, odd = scalar_line(z_parts(minus), z_parts(plane), z_parts(plus))
        beside = [0.5 * (add, sub)[side](even[n], odd[n]) for n in range(6)]
        row = lax.broadcasted_iota(jnp.int32, (CY, NZ), 0)
        ends = scalar_line(z_parts(jnp.where(row == 0, plane[CY - 1:], 0.0)), None, z_parts(jnp.where(row == 1, plane[:1], 0.0)))
        corner = [0.5 * (add, sub)[side](ends[1][n], ends[2][n]) for n in range(6)]
        for n in range(6):
            g_ref[side, n] = beside[n]
            g_ref[2 + side, n] = corner[n]
        for y in range(CY):
            v = [z_ref[i, EDGE[side], y] for i in range(3)]
            gv = times_g([g_ref[side, n, pl.ds(y, 1), :] for n in range(6)], v)
            e = face(side, pl.ds(ex + y, 1))
            for i in range(3):
                put_split(lr_ref, 0, (side * CY + y) * 3 + i, gv[i])
                put_split(lx_ref, side * wide, y * 3 + i, -(e * ux_ref[side, i, y] + vx_ref[side, i, y]))
                put_split(rx_ref, side * wide, y * 3 + i, face(side, pl.ds((i * CY + y) * MODES, MODES)))
        for n, y in enumerate((CY - 1, 0)):
            e = face(side, pl.ds(ex + y, 1))
            for i in range(3):
                put_split(lc_ref, (side * 2 + n) * wide, i, -(e * cu_ref[side, n, i] + cv_ref[side, n, i]))

    k3 = 3 * NZ
    blocks = [raw_ref[0] + contract(lr_ref[...], rr_ref[...]), raw_ref[1]]
    for n in range(2):
        for side in SIDES:
            v = [(cz_ref[pl.ds(n * wide, MODES), pl.ds((side * 3 + i) * NZ, NZ)].astype(jnp.float32)
                  + cz_ref[pl.ds(n * wide + MODES, MODES), pl.ds((side * 3 + i) * NZ, NZ)].astype(jnp.float32)) for i in range(3)]
            gv = times_g([g_ref[2 + side, m, pl.ds(n, 1), :] for m in range(6)], v)
            for i in range(3):
                put_split(lg_ref, n * wide, side * 3 + i, gv[i])
        blocks.append(contract(lg_ref[pl.ds(n * wide, wide), :], cz_ref[pl.ds(n * wide, wide), :]))
    for side in SIDES:
        rows = slice(side * wide, (side + 1) * wide)
        blocks.append(contract(lx_ref[rows], rx_ref[rows]))
        for n, y in enumerate((CY - 1, 0)):
            blocks.append(contract(lc_ref[pl.ds((side * 2 + n) * wide, wide), :], rx_ref[rows, y * k3:(y + 1) * k3]))
    tall = jnp.concatenate([fold(t) for t in blocks], axis=0)
    rows = tall.shape[0]
    tall = jnp.concatenate([tall, jnp.zeros((rows, NZ - wide), jnp.float32)], axis=1)
    lane = lax.broadcasted_iota(jnp.int32, (rows, NZ), 1)
    tall = jnp.where(lane < MODES, tall + pltpu.roll(tall, NZ - MODES, 1), 0.0)
    for shift in (MODES, 2 * MODES, 4 * MODES):
        tall = tall + pltpu.roll(tall, shift, 1)

    groups = cg_ref[...].astype(jnp.float32)
    at_y, at_x = [lax.broadcasted_iota(jnp.int32, groups.shape, axis) for axis in (0, 1)]

    def group_of(step_x, step_y):
        found = jnp.where((at_x == a + step_x) & (at_y == b + step_y), groups, 0.0)
        return jnp.sum(jnp.sum(found, axis=0, keepdims=True), axis=1, keepdims=True)

    here, ahead, behind, above, below = [group_of(*step) for step in ((0, 0), (1, 0), (-1, 0), (0, 1), (0, -1))]
    group = (lax.broadcasted_iota(jnp.int32, (MODES, NZ), 1) // MODES).astype(jnp.float32)

    def placed(entries):
        rows = []
        for g in range(GROUPS):
            total = jnp.zeros((MODES, NZ), jnp.float32)
            for n, r, c in entries:
                total = total + jnp.where(group == jnp.where(r == g, c, -1.0), tall[n * MODES:(n + 1) * MODES], 0.0)
            rows.append(total)
        return jnp.concatenate(rows, axis=0)

    mid = here + GROUPS
    own = placed([(0, here, mid), (1, here, above + GROUPS), (2, above, above + GROUPS), (3, below, below + GROUPS)])
    left = placed([(7, here, behind), (8, above, behind), (9, below, behind)])
    right = placed([(4, here, ahead), (5, above, ahead), (6, below, ahead)])
    half = GROUPS * MODES
    turned = jnp.concatenate([jnp.zeros_like(own), own], axis=0).T
    middle = left + own + turned[half:]
    n_owners, part = out_ref.shape[:2]
    for d in range(n_owners):
        out_ref[d, :, 0:NZ] = middle[d * part:(d + 1) * part]
        out_ref[d, :, NZ:NZ + half] = right[d * part:(d + 1) * part, :half]


def vmem(n):
    return [pl.BlockSpec(memory_space=pltpu.VMEM)] * n


def f32(*shape):
    return jax.ShapeDtypeStruct(shape, jnp.float32)


def shards(modes, region, stiffness, coarse_group):
    levels = jnp.arange(stiffness.shape[0], dtype=jnp.int32)
    e = jnp.sum(jnp.where(region[..., None] == levels, stiffness, 0.0), axis=-1)
    z = jnp.transpose(modes, (1, 2, 3, 0, 4))
    zeros = jnp.zeros((4, NZ), jnp.float32)
    n_gx, n_gy = lax.axis_size("gx"), lax.axis_size("gy")
    upper = jnp.concatenate([z[:, CX - 1].reshape(-1, NZ), e[CX - 1]], axis=0)
    lower = jnp.concatenate([z[:, 0].reshape(-1, NZ), e[0]], axis=0)
    even_strip = lax.axis_index("gx") % 2 == 0
    pay_yp = jnp.concatenate([z[:, :, 0].reshape(-1, NZ), e[:, 0], zeros], axis=0)
    pay_ym = jnp.concatenate([z[:, x, CY - 1].reshape(-1, NZ) for x in EDGE] + [e[:, CY - 1], zeros], axis=0)
    pairs = [[(i, i + 1) for i in range(start, n_gx - 1, 2)] for start in (0, 1)]
    swaps = [p + [(j, i) for i, j in p] for p in pairs]
    first = lax.ppermute(jnp.where(even_strip, upper, lower), "gx", swaps[0])
    second = lax.ppermute(jnp.where(even_strip, lower, upper), "gx", swaps[1])
    got_yp = lax.ppermute(pay_yp, "gy", [(i + 1, i) for i in range(n_gy - 1)])
    got_ym = lax.ppermute(pay_ym, "gy", [(i, i + 1) for i in range(n_gy - 1)])

    col = (MODES, NZ)
    wide = 2 * MODES
    bf16 = jnp.bfloat16
    V = pltpu.VMEM
    q, ux, vx, uy, vy = pl.pallas_call(
        own_kernel,
        out_shape=[f32(wide, wide), f32(2, 3, CY, *col), f32(2, 3, CY, *col), f32(3, CX, *col), f32(3, CX, *col)],
        in_specs=vmem(2),
        out_specs=vmem(5),
        scratch_shapes=[
            V((CX, 3, CY, *col), jnp.float32),
            V((CX, 3, CY, *col), jnp.float32),
            V((CX, 3, CY + 1, *col), jnp.float32),
            V((CX + 1, 3, CY + 1, *col), jnp.float32),
            V((CX + 1, 3, CY + 1, *col), jnp.float32),
            V((CX, 6, CY, NZ), jnp.float32),
            V((wide, 3 * CY * NZ), bf16),
            V((wide, 3 * CY * NZ), bf16),
        ],
        cost_estimate=pl.CostEstimate(flops=4_000_000_000, bytes_accessed=1_000_000, transcendentals=0),
        compiler_params=pltpu.CompilerParams(vmem_limit_bytes=16 * 2**20),
        name="own",
    )(z, e)
    raw, cu, cv, cz = pl.pallas_call(
        y_kernel,
        out_shape=[f32(2, wide, wide), f32(2, 2, 3, *col), f32(2, 2, 3, *col), jax.ShapeDtypeStruct((2 * wide, 6 * NZ), bf16)],
        in_specs=vmem(7),
        out_specs=vmem(4),
        scratch_shapes=[
            V((CX, 6, CY, NZ), jnp.float32),
            V((wide, 3 * CX * NZ), bf16),
            V((wide, 3 * CX * NZ), bf16),
            V((wide, 6 * CX * NZ), bf16),
            V((wide, 6 * CX * NZ), bf16),
        ],
        cost_estimate=pl.CostEstimate(flops=1_000_000_000, bytes_accessed=500_000, transcendentals=0),
        compiler_params=pltpu.CompilerParams(vmem_limit_bytes=16 * 2**20),
        name="beside_y",
    )(z, e, q, uy, vy, got_yp, got_ym)
    parts = pl.pallas_call(
        x_kernel,
        out_shape=f32(n_gy, GROUPS * MODES // n_gy, 3 * GROUPS * MODES),
        in_specs=vmem(10),
        out_specs=pl.BlockSpec(memory_space=pltpu.VMEM),
        scratch_shapes=[
            V((4, 6, CY, NZ), jnp.float32),
            V((2 * wide, 3 * CY * NZ), bf16),
            V((2 * wide, 3 * CY * NZ), bf16),
            V((4 * wide, 3 * NZ), bf16),
            V((2 * wide, 6 * NZ), bf16),
            V((wide, 6 * CY * NZ), bf16),
            V((wide, 6 * CY * NZ), bf16),
        ],
        cost_estimate=pl.CostEstimate(flops=1_000_000_000, bytes_accessed=500_000, transcendentals=0),
        compiler_params=pltpu.CompilerParams(vmem_limit_bytes=16 * 2**20),
        name="beside_x",
    )(coarse_group.T, z, raw, ux, vx, cu, cv, cz, first, second)
    parts = lax.all_to_all(parts, "gy", 0, 0, tiled=True)
    return jnp.sum(parts, axis=0)[None]


def solution(mesh):
    in_specs = (P(None, None, "gx", "gy", None), P("gx", "gy", None), P(), P())
    out_specs = P("gx", "gy", None)
    return jax.shard_map(shards, mesh=mesh, in_specs=in_specs, out_specs=out_specs, check_vma=False)
```

time: 46.1 us -> 35.1 us (0.76)
  Pallas kernels: 8.08 us -> 4.61 us
  waiting for transfers between devices: 6.21 us -> 3.35 us
  starting transfers between devices: 12.9 us -> 11.1 us
  local copies, waits for them, and re-layouts: 3.78 us -> 2.34 us
  other arithmetic: 2.35 us -> 1.52 us
  blocking collectives: 12.2 us -> 11.7 us
    pallas_call x2 -> x3, Pallas kernels: 8.08 us -> 4.61 us  [the longest x1 2.9 us: shards(): pl.pallas_call(own_kernel, out_shape=[f32(wide, wide), f32(2, 3, CY, *col...]
    ppermute x2, waiting for transfers between devices: 6.2 us -> 3.34 us  [the longest x1 2.68 us: shards(): first = lax.ppermute(jnp.where(even_strip, upper, lower), 'gx', swaps[0])]
    ppermute x2, starting transfers between devices: 9.85 us -> 8.04 us  [the longest x1 7.94 us: shards(): second = lax.ppermute(jnp.where(even_strip, lower, upper), 'gx', swaps[1])]
    reshape x1 -> x0, other arithmetic: 0.85 us -> none  [shards(): rows.reshape(n_gy, -1, own.shape[1])]
    unnamed x13 -> x3, local copies, waits for them, and re-layouts: 2.97 us -> 2.28 us
    reshape x1 -> x0, local copies, waits for them, and re-layouts: 0.6 us -> none  [shards(): lax.dynamic_slice(group_pad, (lax.axis_index('gx'), lax.axis_index('gy'))...]
    all_to_all x1, blocking collectives: 12.2 us -> 11.7 us  [shards(): parts = lax.all_to_all(parts, 'gy', 0, 0, tiled=True)]
  transfers between devices with their start and end apart: 4 -> 4, of which waited for: 1 -> 2; matrix products, arithmetic and copies ran while one was open for 2% -> 0% of each run, Pallas kernels for 10% -> 10%
where the time goes in v2:
time: 35.1 us; the launch traced here: 34.8 us
  blocking collectives  11.7 us (33%)
  starting transfers between devices  11.1 us (32%)
  Pallas kernels  4.61 us (13%)
  waiting for transfers between devices  3.35 us (10%)
  local copies, waits for them, and re-layouts  2.34 us (7%)
  other arithmetic  1.52 us (4%)
    all_to_all x1, blocking collectives, shards(): parts = lax.all_to_all(parts, 'gy', 0, 0, tiled=True)  11.7 us
    ppermute x1, starting transfers between devices, shards(): second = lax.ppermute(jnp.where(even_strip, lower, upper), 'gx', swaps[1])  7.94 us
    pallas_call x1, Pallas kernels, shards(): pl.pallas_call(own_kernel, out_shape=[f32(wide, wide), f32(2, 3, CY, *col...  2.9 us
    ppermute x1, waiting for transfers between devices, shards(): first = lax.ppermute(jnp.where(even_strip, upper, lower), 'gx', swaps[0])  2.68 us
    unnamed x3, local copies, waits for them, and re-layouts  2.28 us
    ppermute x1, starting transfers between devices, shards(): got_ym = lax.ppermute(pay_ym, 'gy', [(i, i + 1) for i in range(n_gy - 1)])  1.74 us
    ppermute x1, starting transfers between devices, shards(): got_yp = lax.ppermute(pay_yp, 'gy', [(i + 1, i) for i in range(n_gy - 1)])  1.29 us
    pallas_call x1, Pallas kernels, shards(): pl.pallas_call(x_kernel, out_shape=f32(n_gy, GROUPS * MODES // n_gy, 3 *...  1.29 us
  transfers between devices with their start and end apart: 4, of which 2 were waited for; matrix products, arithmetic and copies ran while one was open for 0% of the time, Pallas kernels for 10%

profile of v2, /device:TPU:24, one launch (start us, length us, event | category | flops | bytes accessed | tf_op | source)
XLA Modules:
  0.0 34.8 jit_solution(12150751253007417186)
XLA Ops:
  0.0 0.9 %select_reduce_fusion.e_ref = f32[4,8,128]{2,1,0:T(8,128)S(1)} fusion(f32[16]{0:T(128)} %param.6, s32[4,8,128]{2,1,0:T(8,128)} %param.5), kind=kLoop, calls=%fused_computation.1 | loop fusion | flops 192512 | bytes 32832 | tf_op jit(solution)/shard_map/reduce_sum | solution.py:381
  0.9 1.6 %copy.12 = f32[16,3,4,8,128]{4,0,3,2,1:T(8,128)S(1)} copy(f32[16,3,4,8,128]{4,3,2,1,0:T(8,128)} %param.4) | data formatting | bytes 1572864 | tf_op args[0]
  2.5 1.7 %collective-permute-start.1 = (f32[104,128]{1,0:T(8,128)S(1)}, f32[104,128]{1,0:T(8,128)S(1)}, u32[]{:S(2)}, u32[]{:S(2)}) collective-permute-start(f32[104,128]{1,0:T(8,128)S(1)} %pad_maximum_fusion.3), channel_id=1, source_target_pairs={{0,1},{1,2},{2,3},{3,4},{4,5},{5,6},{6,7},{8,9},{9,10},{10,11},{11... | collective-permute-start | bytes 159752 | tf_op jit(solution)/shard_map/ppermute | solution.py:395
  4.3 1.3 %collective-permute-start = (f32[200,128]{1,0:T(8,128)S(1)}, f32[200,128]{1,0:T(8,128)S(1)}, u32[]{:S(2)}, u32[]{:S(2)}) collective-permute-start(f32[200,128]{1,0:T(8,128)S(1)} %pad_maximum_fusion.2), channel_id=1, source_target_pairs={{1,0},{2,1},{3,2},{4,3},{5,4},{6,5},{7,6},{9,8},{10,9},{11,10},{12... | collective-permute-start | bytes 307208 | tf_op jit(solution)/shard_map/ppermute | solution.py:394
  5.7 7.9 %collective-permute-start.3 = (f32[392,128]{1,0:T(8,128)S(1)}, f32[392,128]{1,0:T(8,128)S(1)}, u32[]{:S(2)}, u32[]{:S(2)}) collective-permute-start(f32[392,128]{1,0:T(8,128)S(1)} %get-tuple-element.27), channel_id=1, source_target_pairs={{8,16},{24,32},{40,48},{56,64},{72,80},{88,96},{104,112},{120,128}... | collective-permute-start | bytes 602120 | tf_op jit(solution)/shard_map/ppermute | solution.py:393
  13.7 0.1 collective-permute-start.2
  13.8 2.9 %own.1 = (f32[32,32]{1,0:T(8,128)S(1)}, f32[2,3,8,16,128]{4,3,2,1,0:T(8,128)S(1)}, f32[2,3,8,16,128]{4,3,2,1,0:T(8,128)S(1)}, f32[3,4,16,128]{3,2,1,0:T(8,128)S(1)}, f32[3,4,16,128]{3,2,1,0:T(8,128)S(1)}) custom-call(f32[3,4,8,16,128]{4,3,2,1,0:T(8,128)S(1)} %bitcast.23, f32[4,8,128]{2,1,0:T(8,128)S(1)} %select_reduce_fusion.e_ref), custom_call_target="tpu_custom_call" | custom-call | flops 4000000000 | bytes 1000000 | tf_op jit(solution)/shard_map/own/pallas_call | solution.py:401
  16.7 0.0 collective-permute-done.1.ym_ref
  16.7 0.0 collective-permute-done.yp_ref
  16.7 0.4 %beside_y.1 = (f32[2,32,32]{2,1,0:T(8,128)S(1)}, f32[2,2,3,16,128]{4,3,2,1,0:T(8,128)S(1)}, f32[2,2,3,16,128]{4,3,2,1,0:T(8,128)S(1)}, bf16[64,768]{1,0:T(8,128)(2,1)S(1)}) custom-call(f32[3,4,8,16,128]{4,3,2,1,0:T(8,128)S(1)} %bitcast.24, f32[4,8,128]{2,1,0:T(8,128)S(1)} %select_reduce_fusion.e_ref, f32[32,32]{1,0:T(8,128)S(1)} %get-tuple-element.14.q_ref, ...), custom_call_target="tpu_custom_call" | custom-call | flops 1000000000 | bytes 500000 | tf_op jit(solution)/shard_map/beside_y/pallas_call | solution.py:420
  17.1 0.7 %collective-permute-done.3.second_ref = f32[392,128]{1,0:T(8,128)S(1)} collective-permute-done((f32[392,128]{1,0:T(8,128)S(1)}, f32[392,128]{1,0:T(8,128)S(1)}, u32[]{:S(2)}, u32[]{:S(2)}) %collective-permute-start.3) | collective-permute-done | bytes 200736 | tf_op jit(solution)/shard_map/ppermute | solution.py:393
  17.8 2.7 %collective-permute-done.2.first_ref = f32[392,128]{1,0:T(8,128)S(1)} collective-permute-done((f32[392,128]{1,0:T(8,128)S(1)}, f32[392,128]{1,0:T(8,128)S(1)}, u32[]{:S(2)}, u32[]{:S(2)}) %collective-permute-start.2) | collective-permute-done | bytes 200736 | tf_op jit(solution)/shard_map/ppermute | solution.py:392
  20.5 0.0 copy-start
  20.5 0.7 %copy-done = s32[32,8]{0,1:T(8,128)S(1)} copy-done((s32[32,8]{0,1:T(8,128)S(1)}, s32[32,8]{0,1:T(8,128)}, u32[]{:S(2)}) %copy-start) | copy-done | bytes 1048
  21.1 1.3 %beside_x.1 = f32[8,8,192]{2,1,0:T(8,128)S(1)} custom-call(s32[8,32]{1,0:T(8,128)S(1)} %bitcast.26, f32[3,4,8,16,128]{4,3,2,1,0:T(8,128)S(1)} %bitcast.25, f32[2,32,32]{2,1,0:T(8,128)S(1)} %get-tuple-element.17.raw_ref, f32[2,3,8,16,128]{4,3,2,1,0:T(8,128)S(1)} %get-tuple-element.18.ux_ref, f32[2,3,8,16,128]{4,3,2,1,0:T(8,128)S(1)} %get-tuple-element.19.vx_ref, ...), custom_call_target="tpu_custom_call" | custom-call | flops 1000000000 | bytes 500000 | tf_op jit(solution)/shard_map/beside_x/pallas_call | solution.py:436
  22.4 11.7 %all_to_all.5 = f32[8,8,192]{2,1,0:T(8,128)S(1)} all-to-all(f32[8,8,192]{2,1,0:T(8,128)S(1)} %beside_x.1), channel_id=1, replica_groups=mesh['gx'=32,'gy'=8] {'gy'}, dimensions={0} | all-to-all | bytes 98304 | tf_op jit(solution)/shard_map/all_to_all | solution.py:454
  34.2 0.6 %reduce_sum.19 = f32[8,192]{1,0:T(8,128)} reduce(f32[8,8,192]{2,1,0:T(8,128)S(1)} %all_to_all.5, f32[]{:T(128)} %constant.17.clone.1), dimensions={0}, to_apply=%region_1.2 | reduce | flops 10752 | bytes 55300 | tf_op jit(solution)/shard_map/reduce_sum | solution.py:455
  (9 shorter events, 0.1 us)
Async XLA Ops:
  2.5 14.2 %collective-permute-start.1 = (f32[104,128]{1,0:T(8,128)S(1)}, f32[104,128]{1,0:T(8,128)S(1)}, u32[]{:S(2)}, u32[]{:S(2)}) collective-permute-start(f32[104,128]{1,0:T(8,128)S(1)} %pad_maximum_fusion.3), channel_id=1, source_target_pairs={{0,1},{1,2},{2,3},{3,4},{4,5},{5,6},{6,7},{8,9},{9,10},{10,11},{11... | collective-permute-start | bytes 159752 | tf_op jit(solution)/shard_map/ppermute | solution.py:395
  4.3 12.4 %collective-permute-start = (f32[200,128]{1,0:T(8,128)S(1)}, f32[200,128]{1,0:T(8,128)S(1)}, u32[]{:S(2)}, u32[]{:S(2)}) collective-permute-start(f32[200,128]{1,0:T(8,128)S(1)} %pad_maximum_fusion.2), channel_id=1, source_target_pairs={{1,0},{2,1},{3,2},{4,3},{5,4},{6,5},{7,6},{9,8},{10,9},{11,10},{12... | collective-permute-start | bytes 307208 | tf_op jit(solution)/shard_map/ppermute | solution.py:394
  5.7 12.1 %collective-permute-start.3 = (f32[392,128]{1,0:T(8,128)S(1)}, f32[392,128]{1,0:T(8,128)S(1)}, u32[]{:S(2)}, u32[]{:S(2)}) collective-permute-start(f32[392,128]{1,0:T(8,128)S(1)} %get-tuple-element.27), channel_id=1, source_target_pairs={{8,16},{24,32},{40,48},{56,64},{72,80},{88,96},{104,112},{120,128}... | collective-permute-start | bytes 602120 | tf_op jit(solution)/shard_map/ppermute | solution.py:393
  13.7 6.8 %collective-permute-start.2 = (f32[392,128]{1,0:T(8,128)S(1)}, f32[392,128]{1,0:T(8,128)S(1)}, u32[]{:S(2)}, u32[]{:S(2)}) collective-permute-start(f32[392,128]{1,0:T(8,128)S(1)} %get-tuple-element.28), channel_id=1, source_target_pairs={{0,8},{16,24},{32,40},{48,56},{64,72},{80,88},{96,104},{112,120},{... | collective-permute-start | bytes 602120 | tf_op jit(solution)/shard_map/ppermute | solution.py:392
  20.5 0.7 %copy-start = (s32[32,8]{0,1:T(8,128)S(1)}, s32[32,8]{0,1:T(8,128)}, u32[]{:S(2)}) copy-start(s32[32,8]{0,1:T(8,128)} %param.7) | copy-start | bytes 3076
